TPU v7x, 32 devices: a whole 2x2x4 slice. The times are simulated.
32 devices in a mesh: chan: 8 (over z, core), band: 4 (over y, x).
Axes of the slice: x: 2, y: 2, z: 4, core: 2. Of those that a mesh axis runs over, the one named last changes fastest.
Arguments:
- residual: float32 [64, 96, 16384], P('chan', 'band'), may hold values from -60 to 60
- weight_index: int32 [64], P('chan'), may hold values from 0 to 15
- weight_table: float32 [16], replicated, may hold values from 0.2 to 5
- gridded: float32 [2, 8, 128, 16384], P(None, 'chan', 'band'), may hold values from -6 to 6
Outputs:
- components: float32 [3, 96, 16384], P(None, 'band', 'chan')
- spectrum: float32 [2, 8, 16384, 128], P(None, 'chan', 'band')
All inputs are finite; a program needn't handle non-finite values.
Results may differ from a plain program's by a relative error of at most 0.0002.
Values sent between devices are 32-bit elements; how exact they have to be, the bound alone decides.
A program may use at most 128 MiB of HBM per device.

v0:
```python
import functools
import math

import jax
import jax.numpy as jnp
import numpy as np
from jax import lax
from jax.experimental import pallas as pl
from jax.experimental.pallas import tpu as pltpu
from jax.sharding import PartitionSpec as P

MESH = pl.DeviceIdType.MESH
LANES = 128
SUB = 8


def block_form(table):
    real = np.block([[table.real, -table.imag], [table.imag, table.real]]).astype(np.float32)
    high = real.astype(jnp.bfloat16)
    low = (real - high.astype(np.float32)).astype(jnp.bfloat16)
    return np.concatenate([high, low, high], axis=1)


def dft(size):
    grid = np.outer(np.arange(size), np.arange(size)) % size
    return np.exp(-2j * np.pi * grid / size)


def tables(length):
    outer = length // LANES
    turn = np.exp(-2j * np.pi * np.outer(np.arange(outer), np.arange(LANES)) / length)
    turn = turn / math.sqrt(length)
    return (
        block_form(dft(outer)),
        block_form(dft(LANES)),
        turn.real.astype(np.float32),
        turn.imag.astype(np.float32),
    )


def inverse_rows(moment):
    s0, s1, s2, s3, s4 = (moment[j : j + 1, :] for j in range(5))
    aa = s2 * s4 - s3 * s3
    ab = s2 * s3 - s1 * s4
    ac = s1 * s3 - s2 * s2
    bb = s0 * s4 - s2 * s2
    bc = s1 * s2 - s0 * s3
    cc = s0 * s2 - s1 * s1
    determ = s0 * aa + s1 * ab + s2 * ac
    return [entry / determ for entry in (aa, ab, ac, bb, bc, cc)]


def exchange_kernel(
    nc,
    nb,
    idx_ref,
    tab_ref,
    first_ref,
    second_ref,
    turn_re_ref,
    turn_im_ref,
    res_hbm,
    grid_hbm,
    spec_hbm,
    tay_ref,
    mom_ref,
    grid_v,
    out_v,
    res_v,
    part_v,
    mom_own,
    mom_all,
    *rest,
):
    steps = int(math.log2(nc))
    lands = rest[:steps]
    (grid_sem, res_sem, own_sem, fs_sem, fr_sem, rs_sem, rr_sem, ms_sem, mr_sem) = rest[steps:]
    chan = lax.axis_index("chan")
    band = lax.axis_index("band")
    tiles, outer8 = grid_v.shape[1], grid_v.shape[2]
    outer = outer8 // SUB
    rows = tiles * SUB
    kept = LANES // nb
    parts = res_v.shape[0]
    count = res_v.shape[1]
    wide = part_v.shape[3]
    chunks = part_v.shape[0]
    cuts = chunks // parts

    def grid_copy(t):
        return pltpu.make_async_copy(grid_hbm.at[:, t], grid_v.at[:, t], grid_sem.at[t])

    def res_copy(c):
        return pltpu.make_async_copy(
            res_hbm.at[:, pl.ds(c * SUB, SUB), :], res_v.at[c], res_sem.at[c]
        )

    order = max(tiles, parts)
    for i in range(order):
        if i < parts:
            res_copy(i).start()
        if i < tiles:
            grid_copy(i).start()

    barrier = pltpu.get_barrier_semaphore()
    for d in range(1, nc):
        peer = lax.rem(chan + d, nc)
        pl.semaphore_signal(barrier, inc=1, device_id=(peer, band), device_id_type=MESH)
    for d in range(1, nb):
        peer = lax.rem(band + d, nb)
        pl.semaphore_signal(barrier, inc=1, device_id=(chan, peer), device_id_type=MESH)

    total = count * nc
    coeffs = []
    moments = [jnp.float32(0.0)] * 5
    for c in range(count):
        weight = tab_ref[idx_ref[c]]
        position = (chan * count + c).astype(jnp.float32)
        offset = (2.0 * position + 1.0) * (1.0 / total) - 1.0
        power = weight
        trio = []
        for j in range(5):
            if j < 3:
                trio.append(power)
            moments[j] = moments[j] + power
            power = power * offset
        coeffs.append(trio)
    line = lax.broadcasted_iota(jnp.int32, (SUB, LANES), 0)
    tile = jnp.zeros((SUB, LANES), jnp.float32)
    for j in range(5):
        tile = jnp.where(line == j, moments[j], tile)
    mom_own[...] = tile

    def transform(t):
        def pair(i, carry):
            cols = []
            for k in range(2):
                r = i * 2 + k
                cols.append(
                    jnp.concatenate(
                        [grid_v[p, t, pl.ds(r, outer, stride=SUB), :] for p in range(2)], axis=0
                    )
                )
            x = jnp.concatenate(cols, axis=1)
            high = x.astype(jnp.bfloat16)
            low = (x - high.astype(jnp.float32)).astype(jnp.bfloat16)
            mid = jnp.dot(
                first_ref[...],
                jnp.concatenate([high, high, low], axis=0),
                preferred_element_type=jnp.float32,
            )
            turn_re, turn_im = turn_re_ref[...], turn_im_ref[...]
            turned = []
            for k in range(2):
                re = mid[:outer, k * LANES : (k + 1) * LANES]
                im = mid[outer:, k * LANES : (k + 1) * LANES]
                turned.append(
                    jnp.concatenate(
                        [re * turn_re - im * turn_im, re * turn_im + im * turn_re], axis=1
                    )
                )
            y = jnp.concatenate(turned, axis=0)
            high = y.astype(jnp.bfloat16)
            low = (y - high.astype(jnp.float32)).astype(jnp.bfloat16)
            out = lax.dot_general(
                second_ref[...],
                jnp.concatenate([high, high, low], axis=1),
                (((1,), (1,)), ((), ())),
                preferred_element_type=jnp.float32,
            )
            for k in range(2):
                for p in range(2):
                    out_v[p, t * SUB + i * 2 + k] = out[
                        p * LANES : (p + 1) * LANES, k * outer : (k + 1) * outer
                    ]
            return carry

        lax.fori_loop(0, SUB // 2, pair, 0)

    def block_send(t, d):
        peer = lax.rem(band + d, nb)
        return pltpu.make_async_remote_copy(
            src_ref=out_v.at[:, pl.ds(t * SUB, SUB), pl.ds(peer * kept, kept), :],
            dst_ref=spec_hbm.at[:, pl.ds(band * rows + t * SUB, SUB), :, :],
            send_sem=fs_sem.at[t, d - 1],
            recv_sem=fr_sem.at[t, d - 1],
            device_id=(chan, peer),
            device_id_type=MESH,
        )

    def block_keep(t):
        return pltpu.make_async_copy(
            out_v.at[:, pl.ds(t * SUB, SUB), pl.ds(band * kept, kept), :],
            spec_hbm.at[:, pl.ds(band * rows + t * SUB, SUB), :, :],
            own_sem.at[t],
        )

    def weigh(c):
        step = 512 if wide % 512 == 0 else LANES

        def one(j, carry):
            spot = 0
            for s in range(steps):
                spot = spot + ((j // (1 << s)) % 2) * (1 << (steps - 1 - s))
            for q in range(wide // step):
                col = pl.multiple_of((j * cuts + c % cuts) * wide + q * step, LANES)
                sums = [None] * 3
                for ch in range(count):
                    x = res_v[c // cuts, ch, :, pl.ds(col, step)]
                    for t in range(3):
                        term = coeffs[ch][t] * x
                        sums[t] = term if ch == 0 else sums[t] + term
                for t in range(3):
                    part_v[c, spot, pl.ds(t * SUB, SUB), pl.ds(q * step, step)] = sums[t]
            return carry

        lax.fori_loop(0, nc, one, 0)

    bits = [(chan // (1 << s)) % 2 for s in range(steps)]
    partners = [chan + (1 - 2 * bits[s]) * (1 << s) for s in range(steps)]
    starts = [0]
    for s in range(steps):
        starts.append(starts[s] + bits[s] * (nc >> (s + 1)))

    def half_send(c, s):
        size = nc >> (s + 1)
        begin = starts[s] + (1 - bits[s]) * size
        return pltpu.make_async_remote_copy(
            src_ref=part_v.at[c, pl.ds(begin, size)],
            dst_ref=lands[s].at[c],
            send_sem=rs_sem.at[c, s],
            recv_sem=rr_sem.at[c, s],
            device_id=(partners[s], band),
            device_id_type=MESH,
        )

    def half_add(c, s, send=True):
        half_send(c, s).wait_recv()
        size = nc >> (s + 1)
        if s == steps - 1:
            for t in range(3):
                span = pl.ds(t * SUB, SUB)
                tay_ref[t, c // cuts, :, pl.ds(c % cuts * wide, wide)] = part_v[c, starts[s + 1], span, :] + lands[s][c, 0, span, :]
            return
        half = size // 2
        for mine in (1 - bits[s + 1], bits[s + 1]):
            for q in range(half):
                at = mine * half + q
                part_v[c, starts[s + 1] + at] = part_v[c, starts[s + 1] + at] + lands[s][c, at]
            if send and mine is not bits[s + 1]:
                half_send(c, s + 1).start()

    def mom_send(d):
        peer = lax.rem(chan + d, nc)
        return pltpu.make_async_remote_copy(
            src_ref=mom_own,
            dst_ref=mom_all.at[d - 1],
            send_sem=ms_sem.at[d - 1],
            recv_sem=mr_sem.at[d - 1],
            device_id=(peer, band),
            device_id_type=MESH,
        )

    ahead = min(2, chunks)
    moved = 0

    def advance(limit):
        nonlocal moved
        while moved < limit:
            half_add(moved, 1)
            if moved + ahead < chunks:
                half_send(moved + ahead, 1).start()
            moved += 1

    for i in range(order):
        if i < parts:
            res_copy(i).wait()
            for c in range(i * cuts, (i + 1) * cuts):
                weigh(c)
                if c == 0:
                    pl.semaphore_wait(barrier, nc + nb - 2)
                half_send(c, 0).start()
        if i < tiles:
            grid_copy(i).wait()
            transform(i)
            for d in range(1, nb):
                block_send(i, d).start()
            block_keep(i).start()
        if i < parts:
            for c in range(i * cuts, (i + 1) * cuts):
                half_add(c, 0, send=c < ahead)
        if i >= 1:
            advance(min(i, (min(i + 1, parts)) * cuts - ahead))
    for d in range(1, nc):
        mom_send(d).start()
    advance(chunks)
    for s in range(2, steps):
        for c in range(chunks):
            half_add(c, s)
    moment = mom_own[...]
    for d in range(1, nc):
        mom_send(d).wait_recv()
        moment = moment + mom_all[d - 1]
    entries = inverse_rows(moment)
    result = jnp.zeros((SUB, LANES), jnp.float32)
    for j, entry in enumerate(entries):
        result = jnp.where(line == j, entry, result)
    mom_ref[...] = result
    for d in range(1, nc):
        mom_send(d).wait_send()
    for c in range(chunks):
        for s in range(steps):
            half_send(c, s).wait_send()
    for t in range(tiles):
        block_keep(t).wait()
        for d in range(1, nb):
            block_send(t, d).wait()


def turn_kernel(inv_ref, in_ref, tay_ref, out_ref, comp_ref):
    many, outer = in_ref.shape[2], in_ref.shape[3]
    for k in range(many):
        out_ref[0, 0, pl.ds(k * outer, outer), :] = in_ref[0, :, k, :].T
    aa, ab, ac, bb, bc, cc = (inv_ref[j, 0] for j in range(6))
    for t, row in enumerate(((aa, ab, ac), (ab, bb, bc), (ac, bc, cc))):
        comp_ref[t] = row[0] * tay_ref[0] + row[1] * tay_ref[1] + row[2] * tay_ref[2]


def local(nc, nb, residual, weight_index, weight_table, gridded):
    count, row_count, columns = residual.shape
    _, groups, rows, length = gridded.shape
    outer = length // LANES
    tiles, parts = rows // SUB, row_count // SUB
    wide = columns // nc
    halves = 2
    kept = LANES // nb
    steps = int(math.log2(nc))
    view = gridded.reshape(2, tiles, SUB, outer, LANES)
    view = jnp.transpose(view, (0, 1, 3, 2, 4)).reshape(2, tiles, outer * SUB, LANES)
    vmem = pl.BlockSpec(memory_space=pltpu.VMEM)
    smem = pl.BlockSpec(memory_space=pltpu.SMEM)
    hbm = pl.BlockSpec(memory_space=pl.ANY)
    dma = pltpu.SemaphoreType.DMA
    raw, taylor, moment = pl.pallas_call(
        functools.partial(exchange_kernel, nc, nb),
        out_shape=(
            jax.ShapeDtypeStruct((2, nb * rows, kept, outer), jnp.float32),
            jax.ShapeDtypeStruct((3, parts, SUB, wide), jnp.float32),
            jax.ShapeDtypeStruct((SUB, LANES), jnp.float32),
        ),
        in_specs=[smem, smem, vmem, vmem, vmem, vmem, hbm, hbm],
        out_specs=(hbm, vmem, vmem),
        scratch_shapes=[
            pltpu.VMEM((2, tiles, outer * SUB, LANES), jnp.float32),
            pltpu.VMEM((2, rows, LANES, outer), jnp.float32),
            pltpu.VMEM((parts, count, SUB, columns), jnp.float32),
            pltpu.VMEM((parts * halves, nc, 3 * SUB, wide // halves), jnp.float32),
            pltpu.VMEM((SUB, LANES), jnp.float32),
            pltpu.VMEM((nc - 1, SUB, LANES), jnp.float32),
            *[
                pltpu.VMEM((parts * halves, nc >> (s + 1), 3 * SUB, wide // halves), jnp.float32)
                for s in range(steps)
            ],
            dma((tiles,)),
            dma((parts,)),
            dma((tiles,)),
            dma((tiles, nb - 1)),
            dma((tiles, nb - 1)),
            dma((parts * halves, steps)),
            dma((parts * halves, steps)),
            dma((nc - 1,)),
            dma((nc - 1,)),
        ],
        compiler_params=pltpu.CompilerParams(
            collective_id=0, has_side_effects=True, vmem_limit_bytes=60 * 1024 * 1024
        ),
        name="exchange",
    )(weight_index, weight_table, *map(jnp.asarray, tables(length)), residual, view)
    many = min(2 * SUB, kept)
    cuts = 2 * (kept // many)
    piece = pl.BlockSpec(
        (3, row_count, wide // cuts), lambda p, k: (0, 0, p * (kept // many) + k)
    )
    spectrum, components = pl.pallas_call(
        turn_kernel,
        grid=(2, kept // many),
        out_shape=(
            jax.ShapeDtypeStruct((2, 1, kept * outer, nb * rows), jnp.float32),
            jax.ShapeDtypeStruct((3, row_count, wide), jnp.float32),
        ),
        in_specs=[
            smem,
            pl.BlockSpec((1, nb * rows, many, outer), lambda p, k: (p, 0, k, 0)),
            piece,
        ],
        out_specs=(
            pl.BlockSpec((1, 1, many * outer, nb * rows), lambda p, k: (p, 0, k, 0)),
            piece,
        ),
        name="turn",
    )(moment, raw, taylor.reshape(3, row_count, wide))
    return (components, spectrum)


def solution(mesh):
    nc, nb = mesh.shape["chan"], mesh.shape["band"]
    in_specs = (P("chan", "band", None), P("chan"), P(), P(None, "chan", "band", None))
    out_specs = (P(None, "band", "chan"), P(None, "chan", "band", None))
    return jax.shard_map(
        functools.partial(local, nc, nb),
        mesh=mesh,
        in_specs=in_specs,
        out_specs=out_specs,
        check_vma=False,
    )
```

profile of v0, /device:TPU:0, one launch (start us, length us, event | category | flops | bytes accessed | tf_op | source)
XLA Modules:
  0.0 65.7 jit_solution(13005988511802184106)
XLA Ops:
  0.6 58.9 %exchange.1 = (f32[2,128,32,128]{3,2,1,0:T(8,128)}, f32[3,3,8,2048]{3,2,1,0:T(8,128)}, f32[8,128]{1,0:T(8,128)}) custom-call(s32[8]{0:T(128)} %idx_ref.1, f32[16]{0:T(128)} %tab_ref.1, bf16[256,768]{1,0:T(8,128)(2,1)} %constant.6.clone.first_ref.second_ref, bf16[256,768]{1,0:T(8,128)(2,1)} %constant.6.clone.first_ref.second_ref, ...), custom_call_target="tpu_custom_call" | custom-call | tf_op jit(solution)/shard_map/exchange/pallas_call | solution.py:344
  59.6 6.1 %turn.1 = (f32[2,1,4096,128]{3,2,1,0:T(8,128)}, f32[3,24,2048]{2,1,0:T(8,128)}) custom-call(f32[8,128]{1,0:T(8,128)} %get-tuple-element.7.inv_ref, f32[2,128,32,128]{3,2,1,0:T(8,128)} %get-tuple-element.8.in_ref, f32[3,24,2048]{2,1,0:T(8,128)} %bitcast.7), custom_call_target="tpu_custom_call" | custom-call | tf_op jit(solution)/shard_map/turn/pallas_call | solution.py:384
where the time goes:
time: 65.9 us; the launch traced here: 65.7 us
  Pallas kernels  65.1 us (99%)
    pallas_call x1, Pallas kernels, local(): pl.pallas_call(functools.partial(exchange_kernel, nc, nb), out_shape=(jax...  58.9 us
    pallas_call x1, Pallas kernels, local(): pl.pallas_call(turn_kernel, grid=(2, kept // many), out_shape=(jax.ShapeD...  6.14 us

commit v1 on v0

v1 whole, which is shorter than its diff:
```python
import functools
import math

import jax
import jax.numpy as jnp
import numpy as np
from jax import lax
from jax.experimental import pallas as pl
from jax.experimental.pallas import tpu as pltpu
from jax.sharding import PartitionSpec as P

MESH = pl.DeviceIdType.MESH
LANES = 128
SUB = 8
AHEAD = 2


def block_form(table):
    real = np.block([[table.real, -table.imag], [table.imag, table.real]]).astype(np.float32)
    high = real.astype(jnp.bfloat16)
    low = (real - high.astype(np.float32)).astype(jnp.bfloat16)
    return np.concatenate([high, low, high], axis=1)


def dft(size):
    grid = np.outer(np.arange(size), np.arange(size)) % size
    return np.exp(-2j * np.pi * grid / size)


def tables(length):
    outer = length // LANES
    turn = np.exp(-2j * np.pi * np.outer(np.arange(outer), np.arange(LANES)) / length)
    turn = turn / math.sqrt(length)
    bases = [block_form(dft(outer))]
    if outer != LANES:
        bases.append(block_form(dft(LANES)))
    return (np.stack([turn.real, turn.imag]).astype(np.float32), *bases)


def inverse_rows(moment):
    s0, s1, s2, s3, s4 = (moment[j : j + 1, :] for j in range(5))
    aa = s2 * s4 - s3 * s3
    ab = s2 * s3 - s1 * s4
    ac = s1 * s3 - s2 * s2
    bb = s0 * s4 - s2 * s2
    bc = s1 * s2 - s0 * s3
    cc = s0 * s2 - s1 * s1
    determ = s0 * aa + s1 * ab + s2 * ac
    return [entry / determ for entry in (aa, ab, ac, bb, bc, cc)]


def exchange_kernel(nc, nb, bases, idx_ref, tab_ref, *rest):
    steps = int(math.log2(nc))
    tables_hbm, (res_hbm, grid_hbm) = rest[: bases + 1], rest[bases + 1 : bases + 3]
    spec_ref, comp_ref = rest[bases + 3 : bases + 5]
    rest = rest[bases + 5 :]
    tables_v, rest = rest[: bases + 1], rest[bases + 1 :]
    (grid_v, out_v, recv_v, res_v, part_v, mom_v, mom_land) = rest[:7]
    lands = rest[7 : 7 + steps]
    (tab_sem, grid_sem, res_sem, es_sem, er_sem, ls_sem, lr_sem, rs_sem, rr_sem, ms_sem, mr_sem) = rest[7 + steps :]
    turn_v, first_v, second_v = tables_v[0], tables_v[1], tables_v[-1]
    chan = lax.axis_index("chan")
    band = lax.axis_index("band")
    tiles, outer8 = grid_v.shape[1], grid_v.shape[2]
    outer = outer8 // SUB
    kept = LANES // nb
    parts = res_v.shape[0]
    count = res_v.shape[1]
    wide = part_v.shape[3]
    chunks = part_v.shape[0]
    cuts = chunks // parts
    early = tiles // 2
    late = tiles - early
    pieces = head_pieces(tiles)
    slices = ls_sem.shape[0]
    span = kept // slices

    def table_copy(j):
        return pltpu.make_async_copy(tables_hbm[j], tables_v[j], tab_sem.at[j])

    def grid_copy(t):
        return pltpu.make_async_copy(grid_hbm.at[:, t], grid_v.at[:, t], grid_sem.at[t])

    def res_copy(c):
        return pltpu.make_async_copy(
            res_hbm.at[:, pl.ds(c * SUB, SUB), :], res_v.at[c], res_sem.at[c]
        )

    bits = [(chan // (1 << s)) % 2 for s in range(steps)]
    partners = [chan + (1 - 2 * bits[s]) * (1 << s) for s in range(steps)]
    starts = [0]
    for s in range(steps):
        starts.append(starts[s] + bits[s] * (nc >> (s + 1)))

    barrier = pltpu.get_barrier_semaphore()
    for d in range(1, nb):
        peer = lax.rem(band + d, nb)
        pl.semaphore_signal(barrier, inc=1, device_id=(chan, peer), device_id_type=MESH)
    for s in range(steps):
        pl.semaphore_signal(barrier, inc=1, device_id=(partners[s], band), device_id_type=MESH)

    for j in range(bases, -1, -1):
        table_copy(j).start()
    for i in range(max(tiles, parts)):
        if i < tiles:
            grid_copy(i).start()
        if i < parts:
            res_copy(i).start()

    total = count * nc
    coeffs = []
    moments = [jnp.float32(0.0)] * 5
    for c in range(count):
        weight = tab_ref[idx_ref[c]]
        position = (chan * count + c).astype(jnp.float32)
        offset = (2.0 * position + 1.0) * (1.0 / total) - 1.0
        power = weight
        trio = []
        for j in range(5):
            if j < 3:
                trio.append(power)
            moments[j] = moments[j] + power
            power = power * offset
        coeffs.append(trio)
    line = lax.broadcasted_iota(jnp.int32, (SUB, LANES), 0)
    tile = jnp.zeros((SUB, LANES), jnp.float32)
    for j in range(5):
        tile = jnp.where(line == j, moments[j], tile)
    mom_v[0] = tile

    def transform(t, begin, stop):
        def pair(i, carry):
            cols = []
            for k in range(2):
                r = i * 2 + k
                cols.append(
                    jnp.concatenate(
                        [grid_v[p, t, pl.ds(r, outer, stride=SUB), :] for p in range(2)], axis=0
                    )
                )
            x = jnp.concatenate(cols, axis=1)
            high = x.astype(jnp.bfloat16)
            low = (x - high.astype(jnp.float32)).astype(jnp.bfloat16)
            mid = jnp.dot(
                first_v[...],
                jnp.concatenate([high, high, low], axis=0),
                preferred_element_type=jnp.float32,
            )
            turn_re, turn_im = turn_v[0], turn_v[1]
            turned = []
            for k in range(2):
                re = mid[:outer, k * LANES : (k + 1) * LANES]
                im = mid[outer:, k * LANES : (k + 1) * LANES]
                turned.append(
                    jnp.concatenate(
                        [re * turn_re - im * turn_im, re * turn_im + im * turn_re], axis=1
                    )
                )
            y = jnp.concatenate(turned, axis=0)
            high = y.astype(jnp.bfloat16)
            low = (y - high.astype(jnp.float32)).astype(jnp.bfloat16)
            out = lax.dot_general(
                second_v[...],
                jnp.concatenate([high, high, low], axis=1),
                (((1,), (1,)), ((), ())),
                preferred_element_type=jnp.float32,
            )
            flat = out_v.reshape(tiles, LANES * 2 * SUB, outer)
            for k in range(2):
                for p in range(2):
                    flat[t, pl.ds(p * SUB + i * 2 + k, LANES, stride=2 * SUB), :] = out[
                        p * LANES : (p + 1) * LANES, k * outer : (k + 1) * outer
                    ]
            return carry

        lax.fori_loop(begin // 2, stop // 2, pair, 0)

    def piece_send(j, d):
        t, begin, size = pieces[j]
        peer = lax.rem(band + d, nb)
        return pltpu.make_async_remote_copy(
            src_ref=out_v.at[t, pl.ds(peer * kept * 2, kept * 2), pl.ds(begin, size), :],
            dst_ref=recv_v.at[band * tiles + t, :, pl.ds(begin, size), :],
            send_sem=es_sem.at[j, d - 1],
            recv_sem=er_sem.at[j, d - 1],
            device_id=(chan, peer),
            device_id_type=MESH,
        )

    def slice_send(q, d):
        peer = lax.rem(band + d, nb)
        return pltpu.make_async_remote_copy(
            src_ref=out_v.at[pl.ds(early, late), pl.ds((peer * kept + q * span) * 2, span * 2)],
            dst_ref=recv_v.at[pl.ds(band * tiles + early, late), pl.ds(q * span * 2, span * 2)],
            send_sem=ls_sem.at[q, d - 1],
            recv_sem=lr_sem.at[q, d - 1],
            device_id=(chan, peer),
            device_id_type=MESH,
        )

    def keep(t):
        recv_v[band * tiles + t] = out_v[t, pl.ds(band * kept * 2, kept * 2)]

    def flip(q):
        def one(k, carry):
            for p in range(2):
                block = recv_v[:, q * span * 2 + k * 2 + p]
                spec_ref[p, 0, pl.ds(pl.multiple_of((q * span + k) * outer, LANES), outer), :] = block.reshape(
                    nb * tiles * SUB, outer
                ).T
            return carry

        lax.fori_loop(0, span, one, 0, unroll=2 if span % 2 == 0 else 1)

    def weigh(c):
        step = 512 if wide % 512 == 0 else LANES

        def one(j, carry):
            spot = 0
            for s in range(steps):
                spot = spot + ((j // (1 << s)) % 2) * (1 << (steps - 1 - s))
            for q in range(wide // step):
                col = pl.multiple_of((j * cuts + c % cuts) * wide + q * step, LANES)
                sums = [None] * 3
                for ch in range(count):
                    x = res_v[c // cuts, ch, :, pl.ds(col, step)]
                    for t in range(3):
                        term = coeffs[ch][t] * x
                        sums[t] = term if ch == 0 else sums[t] + term
                for t in range(3):
                    part_v[c, spot, pl.ds(t * SUB, SUB), pl.ds(q * step, step)] = sums[t]
            return carry

        lax.fori_loop(0, nc, one, 0)

    def half_send(c, s):
        size = nc >> (s + 1)
        begin = starts[s] + (1 - bits[s]) * size
        return pltpu.make_async_remote_copy(
            src_ref=part_v.at[c, pl.ds(begin, size)],
            dst_ref=lands[s].at[c],
            send_sem=rs_sem.at[c, s],
            recv_sem=rr_sem.at[c, s],
            device_id=(partners[s], band),
            device_id_type=MESH,
        )

    def mom_send(s):
        return pltpu.make_async_remote_copy(
            src_ref=mom_v.at[s],
            dst_ref=mom_land.at[s],
            send_sem=ms_sem.at[s],
            recv_sem=mr_sem.at[s],
            device_id=(partners[s], band),
            device_id_type=MESH,
        )

    solved = []

    def mom_add(s):
        mom_send(s).wait_recv()
        moment = mom_v[s] + mom_land[s]
        if s < steps - 1:
            mom_v[s + 1] = moment
            mom_send(s + 1).start()
            return
        for entry in inverse_rows(moment):
            solved.append(jnp.broadcast_to(entry, (SUB, LANES)))

    def half_add(c, s, send=True):
        half_send(c, s).wait_recv()
        size = nc >> (s + 1)
        if s == steps - 1:
            aa, ab, ac, bb, bc, cc = solved
            table = ((aa, ab, ac), (ab, bb, bc), (ac, bc, cc))
            for q in range(wide // LANES):
                at = pl.ds(q * LANES, LANES)
                tay = [
                    part_v[c, starts[s + 1], pl.ds(t * SUB, SUB), at] + lands[s][c, 0, pl.ds(t * SUB, SUB), at]
                    for t in range(3)
                ]
                for t, row in enumerate(table):
                    comp_ref[t, pl.ds(c // cuts * SUB, SUB), pl.ds(c % cuts * wide + q * LANES, LANES)] = (
                        row[0] * tay[0] + row[1] * tay[1] + row[2] * tay[2]
                    )
            return
        half = size // 2
        for mine in (1 - bits[s + 1], bits[s + 1]):
            for q in range(half):
                at = mine * half + q
                part_v[c, starts[s + 1] + at] = part_v[c, starts[s + 1] + at] + lands[s][c, at]
            if send and mine is not bits[s + 1]:
                half_send(c, s + 1).start()

    ahead = min(AHEAD, chunks)
    moved = 0

    def advance():
        nonlocal moved
        half_add(moved, 1)
        if moved + ahead < chunks:
            half_send(moved + ahead, 1).start()
        moved += 1

    weighed = added = 0

    def spread():
        nonlocal weighed
        c = weighed
        if c < chunks:
            if c % cuts == 0:
                res_copy(c // cuts).wait()
            weigh(c)
            half_send(c, 0).start()
        weighed += 1

    def gather():
        nonlocal added
        if added < min(weighed, chunks):
            half_add(added, 0, send=added < ahead)
            added += 1

    def piece_go(j):
        t, begin, size = pieces[j]
        transform(t, begin, begin + size)
        if j == 0:
            pl.semaphore_wait(barrier, nb - 1 + steps)
        for d in range(1, nb):
            piece_send(j, d).start()

    for j in range(bases, -1, -1):
        table_copy(j).wait()
    grid_copy(0).wait()
    for j, (t, begin, size) in enumerate(pieces):
        if begin == 0 and t > 0:
            grid_copy(t).wait()
        piece_go(j)
        if j == 0:
            mom_send(0).start()
        spread()
        if j > 0:
            gather()
            spread()
        if begin + size == SUB:
            keep(t)
            gather()
    for t in range(early, tiles):
        grid_copy(t).wait()
        transform(t, 0, SUB)
        keep(t)
        spread()
        gather()
    for q in range(slices):
        for d in range(1, nb):
            slice_send(q, d).start()
    while weighed < chunks:
        spread()
    while added < chunks:
        gather()
    for s in range(steps):
        mom_add(s)

    def open_pieces():
        for j in range(len(pieces)):
            for d in range(1, nb):
                piece_send(j, d).wait_recv()

    def flip_go(q):
        for d in range(1, nb):
            slice_send(q, d).wait_recv()
        flip(q)

    when = [(z_time(c, chunks), 0, advance, ()) for c in range(chunks)]
    for s in range(2, steps):
        for c in range(chunks):
            when.append((z_time(c + 1.5 + 2 * (s - 2), chunks) if c < chunks - 1 else 1.0 + s, s, half_add, (c, s)))
    when.append((0.5, 9, open_pieces, ()))
    for q in range(slices):
        when.append((0.5 + 0.5 * (q + 1) / slices, 10, flip_go, (q,)))
    when.sort(key=lambda job: job[:2])
    flips = [job for job in when if job[2] is flip_go]
    when.remove(flips[-1])
    when.append(flips[-1])
    for _, _, work, args in when:
        work(*args)

    for s in range(steps):
        mom_send(s).wait_send()
    for c in range(chunks):
        for s in range(steps):
            half_send(c, s).wait_send()
    for d in range(1, nb):
        for j in range(len(pieces)):
            piece_send(j, d).wait_send()
        for q in range(slices):
            slice_send(q, d).wait_send()


def z_time(c, chunks):
    return 0.25 + 0.6 * c / chunks


def head_pieces(tiles):
    early = tiles // 2
    half = SUB // 2
    return [(0, 0, half), (0, half, half)][: 2 * early] + [(t, 0, SUB) for t in range(1, early)]


def place_kernel(spec_ref, comp_ref, spec_hbm, comp_hbm, sem):
    cuts = sem.shape[0] // 2
    rows = spec_ref.shape[2] // cuts
    copies = [pltpu.make_async_copy(comp_ref, comp_hbm, sem.at[2 * cuts])]
    for p in range(2):
        for k in range(cuts):
            at = (p, 0, pl.ds(k * rows, rows))
            copies.append(pltpu.make_async_copy(spec_ref.at[at], spec_hbm.at[at], sem.at[p * cuts + k]))
    for copy in copies:
        copy.start()
    for copy in copies:
        copy.wait()


def local(nc, nb, residual, weight_index, weight_table, gridded):
    count, row_count, columns = residual.shape
    _, groups, rows, length = gridded.shape
    outer = length // LANES
    tiles, parts = rows // SUB, row_count // SUB
    wide = columns // nc
    halves = 2
    kept = LANES // nb
    slices = min(8, kept)
    steps = int(math.log2(nc))
    view = gridded.reshape(2, tiles, SUB, outer, LANES)
    view = jnp.transpose(view, (0, 1, 3, 2, 4)).reshape(2, tiles, outer * SUB, LANES)
    vmem = pl.BlockSpec(memory_space=pltpu.VMEM)
    smem = pl.BlockSpec(memory_space=pltpu.SMEM)
    hbm = pl.BlockSpec(memory_space=pl.ANY)
    dma = pltpu.SemaphoreType.DMA
    consts = [jnp.asarray(table) for table in tables(length)]
    bases = len(consts) - 1
    pieces = len(head_pieces(tiles))
    shape_spec = (2, 1, kept * outer, nb * rows)
    shape_comp = (3, row_count, wide)
    held = pl.pallas_call(
        functools.partial(exchange_kernel, nc, nb, bases),
        out_shape=(pltpu.VMEM(shape_spec, jnp.float32), pltpu.VMEM(shape_comp, jnp.float32)),
        in_specs=[smem, smem] + [hbm] * (bases + 3),
        out_specs=(vmem, vmem),
        scratch_shapes=[
            *[pltpu.VMEM(c.shape, c.dtype) for c in consts],
            pltpu.VMEM((2, tiles, outer * SUB, LANES), jnp.float32),
            pltpu.VMEM((tiles, LANES * 2, SUB, outer), jnp.float32),
            pltpu.VMEM((nb * tiles, kept * 2, SUB, outer), jnp.float32),
            pltpu.VMEM((parts, count, SUB, columns), jnp.float32),
            pltpu.VMEM((parts * halves, nc, 3 * SUB, wide // halves), jnp.float32),
            pltpu.VMEM((steps, SUB, LANES), jnp.float32),
            pltpu.VMEM((steps, SUB, LANES), jnp.float32),
            *[
                pltpu.VMEM((parts * halves, nc >> (s + 1), 3 * SUB, wide // halves), jnp.float32)
                for s in range(steps)
            ],
            dma((bases + 1,)),
            dma((tiles,)),
            dma((parts,)),
            dma((pieces, nb - 1)),
            dma((pieces, nb - 1)),
            dma((slices, nb - 1)),
            dma((slices, nb - 1)),
            dma((parts * halves, steps)),
            dma((parts * halves, steps)),
            dma((steps,)),
            dma((steps,)),
        ],
        compiler_params=pltpu.CompilerParams(
            collective_id=0, has_side_effects=True, vmem_limit_bytes=62_200_000
        ),
        name="exchange",
    )(weight_index, weight_table, *consts, residual, view)
    cuts = 4
    spectrum, components = pl.pallas_call(
        place_kernel,
        out_shape=(
            jax.ShapeDtypeStruct(shape_spec, jnp.float32),
            jax.ShapeDtypeStruct(shape_comp, jnp.float32),
        ),
        in_specs=[vmem, vmem],
        out_specs=(hbm, hbm),
        scratch_shapes=[dma((2 * cuts + 1,))],
        compiler_params=pltpu.CompilerParams(vmem_limit_bytes=16 * 1024 * 1024),
        name="place",
    )(*held)
    return (components, spectrum)


def solution(mesh):
    nc, nb = mesh.shape["chan"], mesh.shape["band"]
    in_specs = (P("chan", "band", None), P("chan"), P(), P(None, "chan", "band", None))
    out_specs = (P(None, "band", "chan"), P(None, "chan", "band", None))
    return jax.shard_map(
        functools.partial(local, nc, nb),
        mesh=mesh,
        in_specs=in_specs,
        out_specs=out_specs,
        check_vma=False,
    )
```

time: 65.9 us -> 66.9 us (1.015)
  no operation moved by 1% of the time
where the time goes in v1:
time: 66.9 us; the launch traced here: 66.2 us
  Pallas kernels  65.6 us (98%)
    pallas_call x1, Pallas kernels, local(): pl.pallas_call(functools.partial(exchange_kernel, nc, nb, bases), out_sha...  63.3 us
    pallas_call x1, Pallas kernels, local(): pl.pallas_call(place_kernel, out_shape=(jax.ShapeDtypeStruct(shape_spec,...  2.27 us

profile of v1, /device:TPU:0, one launch (start us, length us, event | category | flops | bytes accessed | tf_op | source)
XLA Modules:
  0.0 66.2 jit_solution(17870987187988113519)
XLA Ops:
  0.6 63.3 %exchange.1 = (f32[2,1,4096,128]{3,2,1,0:T(8,128)S(1)}, f32[3,24,2048]{2,1,0:T(8,128)S(1)}) custom-call(s32[8]{0:T(128)} %idx_ref.1, f32[16]{0:T(128)} %tab_ref.1, f32[2,128,128]{2,1,0:T(8,128)} %constant.4.clone.rest_0_, bf16[256,768]{1,0:T(8,128)(2,1)} %constant.5.clone.rest_1_, f32[8,24,16384]{2,1,0:T(8,128)} %rest_2_.1, f32[2,4,1024,128]{3,2,1,0:T(8,128)} %bitcast.5), custom_call_target="tpu_custom_call" | custom-call | tf_op jit(solution)/shard_map/exchange/pallas_call | solution.py:444
  64.0 2.3 %place.1 = (f32[2,1,4096,128]{3,2,1,0:T(8,128)}, f32[3,24,2048]{2,1,0:T(8,128)}) custom-call(f32[2,1,4096,128]{3,2,1,0:T(8,128)S(1)} %get-tuple-element.6.spec_ref, f32[3,24,2048]{2,1,0:T(8,128)S(1)} %get-tuple-element.7.comp_ref), custom_call_target="tpu_custom_call" | custom-call | tf_op jit(solution)/shard_map/place/pallas_call | solution.py:480

commit v2 on v1

--- a/solution.py
+++ b/solution.py
@@ -12,7 +12,7 @@
 MESH = pl.DeviceIdType.MESH
 LANES = 128
 SUB = 8
-AHEAD = 2
+AHEAD = 3
 
 
 def block_form(table):
@@ -49,15 +49,15 @@
     return [entry / determ for entry in (aa, ab, ac, bb, bc, cc)]
 
 
-def exchange_kernel(nc, nb, bases, idx_ref, tab_ref, *rest):
+def exchange_kernel(nc, nb, bases, idx_hbm, tab_hbm, *rest):
     steps = int(math.log2(nc))
     tables_hbm, (res_hbm, grid_hbm) = rest[: bases + 1], rest[bases + 1 : bases + 3]
     spec_ref, comp_ref = rest[bases + 3 : bases + 5]
     rest = rest[bases + 5 :]
     tables_v, rest = rest[: bases + 1], rest[bases + 1 :]
-    (grid_v, out_v, recv_v, res_v, part_v, mom_v, mom_land) = rest[:7]
-    lands = rest[7 : 7 + steps]
-    (tab_sem, grid_sem, res_sem, es_sem, er_sem, ls_sem, lr_sem, rs_sem, rr_sem, ms_sem, mr_sem) = rest[7 + steps :]
+    (idx_ref, tab_ref, grid_v, out_v, recv_v, res_v, part_v, mom_v, mom_land) = rest[:9]
+    lands = rest[9 : 9 + steps]
+    (idx_sem, tab_sem, grid_sem, res_sem, es_sem, er_sem, ls_sem, lr_sem, rs_sem, rr_sem, ms_sem, mr_sem) = rest[9 + steps :]
     turn_v, first_v, second_v = tables_v[0], tables_v[1], tables_v[-1]
     chan = lax.axis_index("chan")
     band = lax.axis_index("band")
@@ -92,6 +92,16 @@
     for s in range(steps):
         starts.append(starts[s] + bits[s] * (nc >> (s + 1)))
 
+    small = [
+        pltpu.make_async_copy(idx_hbm, idx_ref, idx_sem.at[0]),
+        pltpu.make_async_copy(tab_hbm, tab_ref, idx_sem.at[1]),
+    ]
+    for j in range(bases, -1, -1):
+        table_copy(j).start()
+    grid_copy(0).start()
+    for copy in small:
+        copy.start()
+
     barrier = pltpu.get_barrier_semaphore()
     for d in range(1, nb):
         peer = lax.rem(band + d, nb)
@@ -99,14 +109,8 @@
     for s in range(steps):
         pl.semaphore_signal(barrier, inc=1, device_id=(partners[s], band), device_id_type=MESH)
 
-    for j in range(bases, -1, -1):
-        table_copy(j).start()
-    for i in range(max(tiles, parts)):
-        if i < tiles:
-            grid_copy(i).start()
-        if i < parts:
-            res_copy(i).start()
-
+    for copy in small:
+        copy.wait()
     total = count * nc
     coeffs = []
     moments = [jnp.float32(0.0)] * 5
@@ -293,72 +297,72 @@
                 half_send(c, s + 1).start()
 
     ahead = min(AHEAD, chunks)
-    moved = 0
-
-    def advance():
+    moved = weighed = added = 0
+
+    def advance(target):
         nonlocal moved
-        half_add(moved, 1)
-        if moved + ahead < chunks:
-            half_send(moved + ahead, 1).start()
-        moved += 1
-
-    weighed = added = 0
-
-    def spread():
+        while moved < min(target, chunks):
+            half_add(moved, 1)
+            if moved + ahead < chunks:
+                half_send(moved + ahead, 1).start()
+            moved += 1
+
+    def spread(target):
         nonlocal weighed
-        c = weighed
-        if c < chunks:
-            if c % cuts == 0:
-                res_copy(c // cuts).wait()
-            weigh(c)
-            half_send(c, 0).start()
-        weighed += 1
-
-    def gather():
+        while weighed < min(target, chunks):
+            if weighed % cuts == 0:
+                res_copy(weighed // cuts).wait()
+            weigh(weighed)
+            half_send(weighed, 0).start()
+            weighed += 1
+
+    def gather(target):
         nonlocal added
-        if added < min(weighed, chunks):
+        while added < min(target, chunks):
             half_add(added, 0, send=added < ahead)
             added += 1
-
-    def piece_go(j):
-        t, begin, size = pieces[j]
-        transform(t, begin, begin + size)
-        if j == 0:
-            pl.semaphore_wait(barrier, nb - 1 + steps)
-        for d in range(1, nb):
-            piece_send(j, d).start()
 
     for j in range(bases, -1, -1):
         table_copy(j).wait()
     grid_copy(0).wait()
-    for j, (t, begin, size) in enumerate(pieces):
-        if begin == 0 and t > 0:
+    for i in range(max(tiles, parts)):
+        if i < parts:
+            res_copy(i).start()
+        if 0 < i + 1 < tiles:
+            grid_copy(i + 1).start()
+
+    half = SUB // 2
+    ends = {(t, begin + size): j for j, (t, begin, size) in enumerate(pieces)}
+    for unit in range(2 * tiles):
+        t, begin = unit // 2, unit % 2 * half
+        if unit > 1 and begin == 0:
             grid_copy(t).wait()
-        piece_go(j)
-        if j == 0:
+        transform(t, begin, begin + half)
+        if unit == 0:
+            pl.semaphore_wait(barrier, nb - 1 + steps)
             mom_send(0).start()
-        spread()
-        if j > 0:
-            gather()
-            spread()
-        if begin + size == SUB:
+        j = ends.get((t, begin + half))
+        if j is not None:
+            for d in range(1, nb):
+                piece_send(j, d).start()
+        if unit == 0:
+            spread(1)
+            mom_add(0)
+            spread(3)
+            gather(2)
+        else:
+            spread(3 * (unit + 1))
+            gather(3 * (unit + 1) - 1)
+            if unit == 2:
+                mom_add(1)
+            advance((0, 0, 1, 2, 3, 3, 4, 5)[min(unit, 7)])
+        if begin:
             keep(t)
-            gather()
-    for t in range(early, tiles):
-        grid_copy(t).wait()
-        transform(t, 0, SUB)
-        keep(t)
-        spread()
-        gather()
     for q in range(slices):
         for d in range(1, nb):
             slice_send(q, d).start()
-    while weighed < chunks:
-        spread()
-    while added < chunks:
-        gather()
-    for s in range(steps):
-        mom_add(s)
+    spread(chunks)
+    gather(chunks)
 
     def open_pieces():
         for j in range(len(pieces)):
@@ -370,34 +374,37 @@
             slice_send(q, d).wait_recv()
         flip(q)
 
-    when = [(z_time(c, chunks), 0, advance, ()) for c in range(chunks)]
+    def z_due(c):
+        return 7.2 + 38.0 * (c + 1) / chunks
+
+    jobs = [(z_due(c), 1, advance, (c + 1,)) for c in range(moved, chunks)]
     for s in range(2, steps):
+        jobs.append((z_due(0) + s, s, mom_add, (s,)))
         for c in range(chunks):
-            when.append((z_time(c + 1.5 + 2 * (s - 2), chunks) if c < chunks - 1 else 1.0 + s, s, half_add, (c, s)))
-    when.append((0.5, 9, open_pieces, ()))
+            jobs.append((max(z_due(c + 2 * (s - 1)) + 2.4, 45.5 + (s - steps)), s, half_add, (c, s)))
+    jobs.append((28.0, 9, open_pieces, ()))
     for q in range(slices):
-        when.append((0.5 + 0.5 * (q + 1) / slices, 10, flip_go, (q,)))
-    when.sort(key=lambda job: job[:2])
-    flips = [job for job in when if job[2] is flip_go]
-    when.remove(flips[-1])
-    when.append(flips[-1])
-    for _, _, work, args in when:
+        jobs.append((32.0 + 22.5 * (q + 1) / slices, 10, flip_go, (q,)))
+    jobs.sort(key=lambda job: job[:2])
+    for _, _, work, args in jobs:
         work(*args)
 
-    for s in range(steps):
-        mom_send(s).wait_send()
-    for c in range(chunks):
+    def drain_z():
         for s in range(steps):
-            half_send(c, s).wait_send()
-    for d in range(1, nb):
-        for j in range(len(pieces)):
-            piece_send(j, d).wait_send()
-        for q in range(slices):
-            slice_send(q, d).wait_send()
-
-
-def z_time(c, chunks):
-    return 0.25 + 0.6 * c / chunks
+            mom_send(s).wait_send()
+        for c in range(chunks):
+            for s in range(steps):
+                half_send(c, s).wait_send()
+
+    def drain_band():
+        for d in range(1, nb):
+            for j in range(len(pieces)):
+                piece_send(j, d).wait_send()
+            for q in range(slices):
+                slice_send(q, d).wait_send()
+
+    drain_z()
+    drain_band()
 
 
 def head_pieces(tiles):
@@ -426,14 +433,13 @@
     outer = length // LANES
     tiles, parts = rows // SUB, row_count // SUB
     wide = columns // nc
-    halves = 2
+    halves = 4
     kept = LANES // nb
     slices = min(8, kept)
     steps = int(math.log2(nc))
     view = gridded.reshape(2, tiles, SUB, outer, LANES)
     view = jnp.transpose(view, (0, 1, 3, 2, 4)).reshape(2, tiles, outer * SUB, LANES)
     vmem = pl.BlockSpec(memory_space=pltpu.VMEM)
-    smem = pl.BlockSpec(memory_space=pltpu.SMEM)
     hbm = pl.BlockSpec(memory_space=pl.ANY)
     dma = pltpu.SemaphoreType.DMA
     consts = [jnp.asarray(table) for table in tables(length)]
@@ -444,10 +450,12 @@
     held = pl.pallas_call(
         functools.partial(exchange_kernel, nc, nb, bases),
         out_shape=(pltpu.VMEM(shape_spec, jnp.float32), pltpu.VMEM(shape_comp, jnp.float32)),
-        in_specs=[smem, smem] + [hbm] * (bases + 3),
+        in_specs=[hbm] * (bases + 5),
         out_specs=(vmem, vmem),
         scratch_shapes=[
             *[pltpu.VMEM(c.shape, c.dtype) for c in consts],
+            pltpu.SMEM(weight_index.shape, jnp.int32),
+            pltpu.SMEM(weight_table.shape, jnp.float32),
             pltpu.VMEM((2, tiles, outer * SUB, LANES), jnp.float32),
             pltpu.VMEM((tiles, LANES * 2, SUB, outer), jnp.float32),
             pltpu.VMEM((nb * tiles, kept * 2, SUB, outer), jnp.float32),
@@ -459,6 +467,7 @@
                 pltpu.VMEM((parts * halves, nc >> (s + 1), 3 * SUB, wide // halves), jnp.float32)
                 for s in range(steps)
             ],
+            dma((2,)),
             dma((bases + 1,)),
             dma((tiles,)),
             dma((parts,)),

time: 66.9 us -> 56.8 us (0.85)
  Pallas kernels: 65.6 us -> 56 us
    pallas_call x1, Pallas kernels: 63.3 us -> 53.7 us  [local(): pl.pallas_call(functools.partial(exchange_kernel, nc, nb, bases), out_sha...]
where the time goes in v2:
time: 56.8 us; the launch traced here: 56.7 us
  Pallas kernels  56 us (99%)
  between operations  0.64 us (1%)
    pallas_call x1, Pallas kernels, local(): pl.pallas_call(functools.partial(exchange_kernel, nc, nb, bases), out_sha...  53.7 us
    pallas_call x1, Pallas kernels, local(): pl.pallas_call(place_kernel, out_shape=(jax.ShapeDtypeStruct(shape_spec,...  2.27 us

profile of v2, /device:TPU:0, one launch (start us, length us, event | category | flops | bytes accessed | tf_op | source)
XLA Modules:
  0.0 56.7 jit_solution(10579549798243262890)
XLA Ops:
  0.6 53.7 %exchange.1 = (f32[2,1,4096,128]{3,2,1,0:T(8,128)S(1)}, f32[3,24,2048]{2,1,0:T(8,128)S(1)}) custom-call(s32[8]{0:T(128)} %idx_hbm.1, f32[16]{0:T(128)} %tab_hbm.1, f32[2,128,128]{2,1,0:T(8,128)} %constant.4.clone.rest_0_, bf16[256,768]{1,0:T(8,128)(2,1)} %constant.5.clone.rest_1_, f32[8,24,16384]{2,1,0:T(8,128)} %rest_2_.1, f32[2,4,1024,128]{3,2,1,0:T(8,128)} %bitcast.5), custom_call_target="tpu_custom_call" | custom-call | tf_op jit(solution)/shard_map/exchange/pallas_call | solution.py:450
  54.4 2.3 %place.1 = (f32[2,1,4096,128]{3,2,1,0:T(8,128)}, f32[3,24,2048]{2,1,0:T(8,128)}) custom-call(f32[2,1,4096,128]{3,2,1,0:T(8,128)S(1)} %get-tuple-element.6.spec_ref, f32[3,24,2048]{2,1,0:T(8,128)S(1)} %get-tuple-element.7.comp_ref), custom_call_target="tpu_custom_call" | custom-call | tf_op jit(solution)/shard_map/place/pallas_call | solution.py:489

commit v3 on v2

--- a/solution.py
+++ b/solution.py
@@ -52,12 +52,12 @@
 def exchange_kernel(nc, nb, bases, idx_hbm, tab_hbm, *rest):
     steps = int(math.log2(nc))
     tables_hbm, (res_hbm, grid_hbm) = rest[: bases + 1], rest[bases + 1 : bases + 3]
-    spec_ref, comp_ref = rest[bases + 3 : bases + 5]
-    rest = rest[bases + 5 :]
+    spec_ref, comp_ref, recv_v = rest[bases + 3 : bases + 6]
+    rest = rest[bases + 6 :]
     tables_v, rest = rest[: bases + 1], rest[bases + 1 :]
-    (idx_ref, tab_ref, grid_v, out_v, recv_v, res_v, part_v, mom_v, mom_land) = rest[:9]
-    lands = rest[9 : 9 + steps]
-    (idx_sem, tab_sem, grid_sem, res_sem, es_sem, er_sem, ls_sem, lr_sem, rs_sem, rr_sem, ms_sem, mr_sem) = rest[9 + steps :]
+    (idx_ref, tab_ref, grid_v, out_v, res_v, part_v, mom_v, mom_land) = rest[:8]
+    lands = rest[8 : 8 + steps]
+    (idx_sem, tab_sem, grid_sem, res_sem, bs_sem, er_sem, lr_sem, rs_sem, rr_sem, ms_sem, mr_sem) = rest[8 + steps :]
     turn_v, first_v, second_v = tables_v[0], tables_v[1], tables_v[-1]
     chan = lax.axis_index("chan")
     band = lax.axis_index("band")
@@ -72,7 +72,7 @@
     early = tiles // 2
     late = tiles - early
     pieces = head_pieces(tiles)
-    slices = ls_sem.shape[0]
+    slices = lr_sem.shape[0]
     span = kept // slices
 
     def table_copy(j):
@@ -88,6 +88,7 @@
 
     bits = [(chan // (1 << s)) % 2 for s in range(steps)]
     partners = [chan + (1 - 2 * bits[s]) * (1 << s) for s in range(steps)]
+    others = [crossed(band, nb, mask) for mask in range(nb - 1, 0, -1)]
     starts = [0]
     for s in range(steps):
         starts.append(starts[s] + bits[s] * (nc >> (s + 1)))
@@ -103,34 +104,10 @@
         copy.start()
 
     barrier = pltpu.get_barrier_semaphore()
-    for d in range(1, nb):
-        peer = lax.rem(band + d, nb)
+    for peer in others:
         pl.semaphore_signal(barrier, inc=1, device_id=(chan, peer), device_id_type=MESH)
     for s in range(steps):
         pl.semaphore_signal(barrier, inc=1, device_id=(partners[s], band), device_id_type=MESH)
-
-    for copy in small:
-        copy.wait()
-    total = count * nc
-    coeffs = []
-    moments = [jnp.float32(0.0)] * 5
-    for c in range(count):
-        weight = tab_ref[idx_ref[c]]
-        position = (chan * count + c).astype(jnp.float32)
-        offset = (2.0 * position + 1.0) * (1.0 / total) - 1.0
-        power = weight
-        trio = []
-        for j in range(5):
-            if j < 3:
-                trio.append(power)
-            moments[j] = moments[j] + power
-            power = power * offset
-        coeffs.append(trio)
-    line = lax.broadcasted_iota(jnp.int32, (SUB, LANES), 0)
-    tile = jnp.zeros((SUB, LANES), jnp.float32)
-    for j in range(5):
-        tile = jnp.where(line == j, moments[j], tile)
-    mom_v[0] = tile
 
     def transform(t, begin, stop):
         def pair(i, carry):
@@ -179,25 +156,23 @@
 
         lax.fori_loop(begin // 2, stop // 2, pair, 0)
 
-    def piece_send(j, d):
+    def piece_send(j, peer):
         t, begin, size = pieces[j]
-        peer = lax.rem(band + d, nb)
         return pltpu.make_async_remote_copy(
             src_ref=out_v.at[t, pl.ds(peer * kept * 2, kept * 2), pl.ds(begin, size), :],
             dst_ref=recv_v.at[band * tiles + t, :, pl.ds(begin, size), :],
-            send_sem=es_sem.at[j, d - 1],
-            recv_sem=er_sem.at[j, d - 1],
+            send_sem=bs_sem.at[0],
+            recv_sem=er_sem.at[0],
             device_id=(chan, peer),
             device_id_type=MESH,
         )
 
-    def slice_send(q, d):
-        peer = lax.rem(band + d, nb)
+    def slice_send(q, peer):
         return pltpu.make_async_remote_copy(
             src_ref=out_v.at[pl.ds(early, late), pl.ds((peer * kept + q * span) * 2, span * 2)],
             dst_ref=recv_v.at[pl.ds(band * tiles + early, late), pl.ds(q * span * 2, span * 2)],
-            send_sem=ls_sem.at[q, d - 1],
-            recv_sem=lr_sem.at[q, d - 1],
+            send_sem=bs_sem.at[0],
+            recv_sem=lr_sem.at[q],
             device_id=(chan, peer),
             device_id_type=MESH,
         )
@@ -206,15 +181,9 @@
         recv_v[band * tiles + t] = out_v[t, pl.ds(band * kept * 2, kept * 2)]
 
     def flip(q):
-        def one(k, carry):
-            for p in range(2):
-                block = recv_v[:, q * span * 2 + k * 2 + p]
-                spec_ref[p, 0, pl.ds(pl.multiple_of((q * span + k) * outer, LANES), outer), :] = block.reshape(
-                    nb * tiles * SUB, outer
-                ).T
-            return carry
-
-        lax.fori_loop(0, span, one, 0, unroll=2 if span % 2 == 0 else 1)
+        flip_slice(recv_v, spec_ref, q * span, span)
+
+    coeffs = []
 
     def weigh(c):
         step = 512 if wide % 512 == 0 else LANES
@@ -237,14 +206,24 @@
 
         lax.fori_loop(0, nc, one, 0)
 
+    batches = batch_list(chunks, steps)
+
+    def batch_of(c, s):
+        for spot, (step, first, last) in enumerate(batches):
+            if step == s and first <= c < last:
+                return spot, first, last
+
+    def landed(ref, sem):
+        pltpu.make_async_copy(ref, ref, sem).wait()
+
     def half_send(c, s):
         size = nc >> (s + 1)
         begin = starts[s] + (1 - bits[s]) * size
         return pltpu.make_async_remote_copy(
             src_ref=part_v.at[c, pl.ds(begin, size)],
             dst_ref=lands[s].at[c],
-            send_sem=rs_sem.at[c, s],
-            recv_sem=rr_sem.at[c, s],
+            send_sem=rs_sem.at[0],
+            recv_sem=rr_sem.at[batch_of(c, s)[0]],
             device_id=(partners[s], band),
             device_id_type=MESH,
         )
@@ -253,7 +232,7 @@
         return pltpu.make_async_remote_copy(
             src_ref=mom_v.at[s],
             dst_ref=mom_land.at[s],
-            send_sem=ms_sem.at[s],
+            send_sem=ms_sem.at[0],
             recv_sem=mr_sem.at[s],
             device_id=(partners[s], band),
             device_id_type=MESH,
@@ -272,7 +251,9 @@
             solved.append(jnp.broadcast_to(entry, (SUB, LANES)))
 
     def half_add(c, s, send=True):
-        half_send(c, s).wait_recv()
+        spot, first, last = batch_of(c, s)
+        if c == first:
+            landed(lands[s].at[pl.ds(first, last - first)], rr_sem.at[spot])
         size = nc >> (s + 1)
         if s == steps - 1:
             aa, ab, ac, bb, bc, cc = solved
@@ -298,14 +279,16 @@
 
     ahead = min(AHEAD, chunks)
     moved = weighed = added = 0
-
-    def advance(target):
-        nonlocal moved
+    issued = ahead
+
+    def advance(target, ahead=AHEAD):
+        nonlocal moved, issued
         while moved < min(target, chunks):
             half_add(moved, 1)
-            if moved + ahead < chunks:
-                half_send(moved + ahead, 1).start()
             moved += 1
+            while issued < min(moved + ahead, chunks):
+                half_send(issued, 1).start()
+                issued += 1
 
     def spread(target):
         nonlocal weighed
@@ -331,7 +314,30 @@
         if 0 < i + 1 < tiles:
             grid_copy(i + 1).start()
 
+    for copy in small:
+        copy.wait()
+    total = count * nc
+    moments = [jnp.float32(0.0)] * 5
+    for c in range(count):
+        weight = tab_ref[idx_ref[c]]
+        position = (chan * count + c).astype(jnp.float32)
+        offset = (2.0 * position + 1.0) * (1.0 / total) - 1.0
+        power = weight
+        trio = []
+        for j in range(5):
+            if j < 3:
+                trio.append(power)
+            moments[j] = moments[j] + power
+            power = power * offset
+        coeffs.append(trio)
+    line = lax.broadcasted_iota(jnp.int32, (SUB, LANES), 0)
+    tile = jnp.zeros((SUB, LANES), jnp.float32)
+    for j in range(5):
+        tile = jnp.where(line == j, moments[j], tile)
+    mom_v[0] = tile
+
     half = SUB // 2
+    goals = [last for step, _, last in batches if step == 0]
     ends = {(t, begin + size): j for j, (t, begin, size) in enumerate(pieces)}
     for unit in range(2 * tiles):
         t, begin = unit // 2, unit % 2 * half
@@ -343,41 +349,39 @@
             mom_send(0).start()
         j = ends.get((t, begin + half))
         if j is not None:
-            for d in range(1, nb):
-                piece_send(j, d).start()
+            for peer in others:
+                piece_send(j, peer).start()
         if unit == 0:
-            spread(1)
+            spread(goals[0])
             mom_add(0)
-            spread(3)
-            gather(2)
+            spread(goals[1])
+            gather(goals[1])
         else:
-            spread(3 * (unit + 1))
-            gather(3 * (unit + 1) - 1)
+            gather(goals[min(unit, len(goals) - 1)])
+            spread(goals[min(unit + 1, len(goals) - 1)])
             if unit == 2:
                 mom_add(1)
             advance((0, 0, 1, 2, 3, 3, 4, 5)[min(unit, 7)])
         if begin:
             keep(t)
     for q in range(slices):
-        for d in range(1, nb):
-            slice_send(q, d).start()
+        for peer in others:
+            slice_send(q, peer).start()
     spread(chunks)
     gather(chunks)
 
     def open_pieces():
-        for j in range(len(pieces)):
-            for d in range(1, nb):
-                piece_send(j, d).wait_recv()
+        landed(recv_v.at[pl.ds(0, (nb - 1) * early)], er_sem.at[0])
 
     def flip_go(q):
-        for d in range(1, nb):
-            slice_send(q, d).wait_recv()
-        flip(q)
+        landed(recv_v.at[pl.ds(0, (nb - 1) * late), pl.ds(0, span * 2)], lr_sem.at[q])
+        if q < slices - 1:
+            flip(q)
 
     def z_due(c):
         return 7.2 + 38.0 * (c + 1) / chunks
 
-    jobs = [(z_due(c), 1, advance, (c + 1,)) for c in range(moved, chunks)]
+    jobs = [(z_due(c), 1, advance, (c + 1, 2)) for c in range(moved, chunks)]
     for s in range(2, steps):
         jobs.append((z_due(0) + s, s, mom_add, (s,)))
         for c in range(chunks):
@@ -390,21 +394,43 @@
         work(*args)
 
     def drain_z():
-        for s in range(steps):
-            mom_send(s).wait_send()
-        for c in range(chunks):
-            for s in range(steps):
-                half_send(c, s).wait_send()
+        landed(mom_v, ms_sem.at[0])
+        landed(part_v.at[:, pl.ds(0, nc - 1)], rs_sem.at[0])
 
     def drain_band():
-        for d in range(1, nb):
-            for j in range(len(pieces)):
-                piece_send(j, d).wait_send()
-            for q in range(slices):
-                slice_send(q, d).wait_send()
+        landed(recv_v.at[pl.ds(0, (nb - 1) * tiles)], bs_sem.at[0])
 
     drain_z()
     drain_band()
+
+
+def crossed(index, size, mask):
+    peer = 0
+    for bit in range(int(math.log2(size))):
+        own = (index // (1 << bit)) % 2
+        peer = peer + (1 - own if mask >> bit & 1 else own) * (1 << bit)
+    return peer
+
+
+def flip_slice(recv_v, spec_ref, first, span):
+    rows, outer = recv_v.shape[0] * SUB, recv_v.shape[3]
+
+    def one(k, carry):
+        for p in range(2):
+            block = recv_v[:, (first + k) * 2 + p].reshape(rows, outer)
+            spec_ref[p, 0, pl.ds(pl.multiple_of((first + k) * outer, LANES), outer), :] = block.T
+        return carry
+
+    lax.fori_loop(0, span, one, 0, unroll=2 if span % 2 == 0 else 1)
+
+
+def batch_list(chunks, steps):
+    batches = [(0, 0, 1), (0, 1, min(3, chunks))]
+    batches += [(0, c, min(c + 3, chunks)) for c in range(3, chunks, 3)]
+    for s in range(1, steps - 1):
+        batches += [(s, c, c + 1) for c in range(chunks)]
+    cuts = sorted({0, max(chunks - 4, 0), chunks - 1, chunks})
+    return batches + [(steps - 1, a, b) for a, b in zip(cuts, cuts[1:])]
 
 
 def head_pieces(tiles):
@@ -413,16 +439,24 @@
     return [(0, 0, half), (0, half, half)][: 2 * early] + [(t, 0, SUB) for t in range(1, early)]
 
 
-def place_kernel(spec_ref, comp_ref, spec_hbm, comp_hbm, sem):
-    cuts = sem.shape[0] // 2
-    rows = spec_ref.shape[2] // cuts
-    copies = [pltpu.make_async_copy(comp_ref, comp_hbm, sem.at[2 * cuts])]
-    for p in range(2):
-        for k in range(cuts):
-            at = (p, 0, pl.ds(k * rows, rows))
-            copies.append(pltpu.make_async_copy(spec_ref.at[at], spec_hbm.at[at], sem.at[p * cuts + k]))
+def place_kernel(slices, spec_ref, comp_ref, recv_ref, spec_hbm, comp_hbm, spec_v, sem):
+    rows = spec_ref.shape[2] // slices
+    ready = rows * (slices - 1)
+    span = recv_ref.shape[1] // 2 // slices
+    copies = [
+        pltpu.make_async_copy(spec_ref.at[p, 0, pl.ds(0, ready)], spec_hbm.at[p, 0, pl.ds(0, ready)], sem.at[p])
+        for p in range(2)
+    ]
+    copies.append(pltpu.make_async_copy(comp_ref, comp_hbm, sem.at[2]))
     for copy in copies:
         copy.start()
+    many, outer = recv_ref.shape[0] * SUB, recv_ref.shape[3]
+    for k in range(span):
+        for p in range(2):
+            block = recv_ref[:, (span * (slices - 1) + k) * 2 + p].reshape(many, outer)
+            spec_v[p, pl.ds(k * outer, outer), :] = block.T
+    copies.append(pltpu.make_async_copy(spec_v, spec_hbm.at[:, 0, pl.ds(ready, rows)], sem.at[3]))
+    copies[-1].start()
     for copy in copies:
         copy.wait()
 
@@ -444,21 +478,21 @@
     dma = pltpu.SemaphoreType.DMA
     consts = [jnp.asarray(table) for table in tables(length)]
     bases = len(consts) - 1
-    pieces = len(head_pieces(tiles))
     shape_spec = (2, 1, kept * outer, nb * rows)
     shape_comp = (3, row_count, wide)
+    shape_recv = (nb * tiles, kept * 2, SUB, outer)
+    batches = len(batch_list(parts * halves, steps))
     held = pl.pallas_call(
         functools.partial(exchange_kernel, nc, nb, bases),
-        out_shape=(pltpu.VMEM(shape_spec, jnp.float32), pltpu.VMEM(shape_comp, jnp.float32)),
+        out_shape=tuple(pltpu.VMEM(shape, jnp.float32) for shape in (shape_spec, shape_comp, shape_recv)),
         in_specs=[hbm] * (bases + 5),
-        out_specs=(vmem, vmem),
+        out_specs=(vmem, vmem, vmem),
         scratch_shapes=[
             *[pltpu.VMEM(c.shape, c.dtype) for c in consts],
             pltpu.SMEM(weight_index.shape, jnp.int32),
             pltpu.SMEM(weight_table.shape, jnp.float32),
             pltpu.VMEM((2, tiles, outer * SUB, LANES), jnp.float32),
             pltpu.VMEM((tiles, LANES * 2, SUB, outer), jnp.float32),
-            pltpu.VMEM((nb * tiles, kept * 2, SUB, outer), jnp.float32),
             pltpu.VMEM((parts, count, SUB, columns), jnp.float32),
             pltpu.VMEM((parts * halves, nc, 3 * SUB, wide // halves), jnp.float32),
             pltpu.VMEM((steps, SUB, LANES), jnp.float32),
@@ -471,30 +505,31 @@
             dma((bases + 1,)),
             dma((tiles,)),
             dma((parts,)),
-            dma((pieces, nb - 1)),
-            dma((pieces, nb - 1)),
-            dma((slices, nb - 1)),
-            dma((slices, nb - 1)),
-            dma((parts * halves, steps)),
-            dma((parts * halves, steps)),
-            dma((steps,)),
+            dma((1,)),
+            dma((1,)),
+            dma((slices,)),
+            dma((1,)),
+            dma((batches,)),
+            dma((1,)),
             dma((steps,)),
         ],
         compiler_params=pltpu.CompilerParams(
-            collective_id=0, has_side_effects=True, vmem_limit_bytes=62_200_000
+            collective_id=0, has_side_effects=True, vmem_limit_bytes=58_000_000
         ),
         name="exchange",
     )(weight_index, weight_table, *consts, residual, view)
-    cuts = 4
     spectrum, components = pl.pallas_call(
-        place_kernel,
+        functools.partial(place_kernel, slices),
         out_shape=(
             jax.ShapeDtypeStruct(shape_spec, jnp.float32),
             jax.ShapeDtypeStruct(shape_comp, jnp.float32),
         ),
-        in_specs=[vmem, vmem],
+        in_specs=[vmem, vmem, vmem],
         out_specs=(hbm, hbm),
-        scratch_shapes=[dma((2 * cuts + 1,))],
+        scratch_shapes=[
+            pltpu.VMEM((2, kept * outer // slices, nb * rows), jnp.float32),
+            dma((4,)),
+        ],
         compiler_params=pltpu.CompilerParams(vmem_limit_bytes=16 * 1024 * 1024),
         name="place",
     )(*held)

time: 56.8 us -> 55.4 us (0.975)
  Pallas kernels: 56 us -> 54.6 us
    pallas_call x1, Pallas kernels: 53.7 us -> 52.4 us  [local(): pl.pallas_call(functools.partial(exchange_kernel, nc, nb, bases), out_sha...]
where the time goes in v3:
time: 55.4 us; the launch traced here: 55.3 us
  Pallas kernels  54.6 us (99%)
  between operations  0.64 us (1%)
    pallas_call x1, Pallas kernels, local(): pl.pallas_call(functools.partial(exchange_kernel, nc, nb, bases), out_sha...  52.4 us
    pallas_call x1, Pallas kernels, local(): pl.pallas_call(functools.partial(place_kernel, slices), out_shape=(jax.Sh...  2.23 us

profile of v3, /device:TPU:0, one launch (start us, length us, event | category | flops | bytes accessed | tf_op | source)
XLA Modules:
  0.0 55.3 jit_solution(10831322852968896029)
XLA Ops:
  0.6 52.4 %exchange.1 = (f32[2,1,4096,128]{3,2,1,0:T(8,128)S(1)}, f32[3,24,2048]{2,1,0:T(8,128)S(1)}, f32[16,64,8,128]{3,2,1,0:T(8,128)S(1)}) custom-call(s32[8]{0:T(128)} %idx_hbm.1, f32[16]{0:T(128)} %tab_hbm.1, f32[2,128,128]{2,1,0:T(8,128)} %constant.4.clone.rest_0_, bf16[256,768]{1,0:T(8,128)(2,1)} %constant.5.clone.rest_1_, f32[8,24,16384]{2,1,0:T(8,128)} %rest_2_.1, ...), custom_call_target="tpu_custom_call" | custom-call | tf_op jit(solution)/shard_map/exchange/pallas_call | solution.py:485
  53.0 2.2 %place.1 = (f32[2,1,4096,128]{3,2,1,0:T(8,128)}, f32[3,24,2048]{2,1,0:T(8,128)}) custom-call(f32[2,1,4096,128]{3,2,1,0:T(8,128)S(1)} %get-tuple-element.7.spec_ref, f32[3,24,2048]{2,1,0:T(8,128)S(1)} %get-tuple-element.8.comp_ref, f32[16,64,8,128]{3,2,1,0:T(8,128)S(1)} %get-tuple-element.9.recv_ref), custom_call_target="tpu_custom_call" | custom-call | tf_op jit(solution)/shard_map/place/pallas_call | solution.py:521

commit v4 on v3

--- a/solution.py
+++ b/solution.py
@@ -13,6 +13,7 @@
 LANES = 128
 SUB = 8
 AHEAD = 3
+HEAD = 2
 
 
 def block_form(table):
@@ -61,11 +62,9 @@
     turn_v, first_v, second_v = tables_v[0], tables_v[1], tables_v[-1]
     chan = lax.axis_index("chan")
     band = lax.axis_index("band")
-    tiles, outer8 = grid_v.shape[1], grid_v.shape[2]
-    outer = outer8 // SUB
+    tiles, outer = grid_v.shape[1], grid_v.shape[2]
     kept = LANES // nb
-    parts = res_v.shape[0]
-    count = res_v.shape[1]
+    count, parts = res_v.shape[0], res_v.shape[1]
     wide = part_v.shape[3]
     chunks = part_v.shape[0]
     cuts = chunks // parts
@@ -78,13 +77,15 @@
     def table_copy(j):
         return pltpu.make_async_copy(tables_hbm[j], tables_v[j], tab_sem.at[j])
 
-    def grid_copy(t):
-        return pltpu.make_async_copy(grid_hbm.at[:, t], grid_v.at[:, t], grid_sem.at[t])
-
-    def res_copy(c):
-        return pltpu.make_async_copy(
-            res_hbm.at[:, pl.ds(c * SUB, SUB), :], res_v.at[c], res_sem.at[c]
-        )
+    def grid_copy(j):
+        first, count, begin, size = grid_reads(tiles)[j]
+        at = (slice(None), pl.ds(first, count), slice(None), pl.ds(begin, size))
+        return pltpu.make_async_copy(grid_hbm.at[at], grid_v.at[at], grid_sem.at[j])
+
+    def res_copy(j):
+        first, count = res_reads(parts)[j]
+        at = pl.ds(first, count)
+        return pltpu.make_async_copy(res_hbm.at[:, at], res_v.at[:, at], res_sem.at[j])
 
     bits = [(chan // (1 << s)) % 2 for s in range(steps)]
     partners = [chan + (1 - 2 * bits[s]) * (1 << s) for s in range(steps)]
@@ -111,12 +112,13 @@
 
     def transform(t, begin, stop):
         def pair(i, carry):
+            grid_flat = grid_v.reshape(2, tiles, outer * SUB, LANES)
             cols = []
             for k in range(2):
                 r = i * 2 + k
                 cols.append(
                     jnp.concatenate(
-                        [grid_v[p, t, pl.ds(r, outer, stride=SUB), :] for p in range(2)], axis=0
+                        [grid_flat[p, t, pl.ds(r, outer, stride=SUB), :] for p in range(2)], axis=0
                     )
                 )
             x = jnp.concatenate(cols, axis=1)
@@ -196,7 +198,7 @@
                 col = pl.multiple_of((j * cuts + c % cuts) * wide + q * step, LANES)
                 sums = [None] * 3
                 for ch in range(count):
-                    x = res_v[c // cuts, ch, :, pl.ds(col, step)]
+                    x = res_v[ch, c // cuts, :, pl.ds(col, step)]
                     for t in range(3):
                         term = coeffs[ch][t] * x
                         sums[t] = term if ch == 0 else sums[t] + term
@@ -293,8 +295,9 @@
     def spread(target):
         nonlocal weighed
         while weighed < min(target, chunks):
-            if weighed % cuts == 0:
-                res_copy(weighed // cuts).wait()
+            for j, (first, _) in enumerate(res_reads(parts)):
+                if weighed == first * cuts:
+                    res_copy(j).wait()
             weigh(weighed)
             half_send(weighed, 0).start()
             weighed += 1
@@ -308,11 +311,12 @@
     for j in range(bases, -1, -1):
         table_copy(j).wait()
     grid_copy(0).wait()
-    for i in range(max(tiles, parts)):
-        if i < parts:
-            res_copy(i).start()
-        if 0 < i + 1 < tiles:
-            grid_copy(i + 1).start()
+    grids, reads = len(grid_reads(tiles)), len(res_reads(parts))
+    for j in range(max(grids - 1, reads)):
+        if j + 1 < grids:
+            grid_copy(j + 1).start()
+        if j < reads:
+            res_copy(j).start()
 
     for copy in small:
         copy.wait()
@@ -341,16 +345,21 @@
     ends = {(t, begin + size): j for j, (t, begin, size) in enumerate(pieces)}
     for unit in range(2 * tiles):
         t, begin = unit // 2, unit % 2 * half
-        if unit > 1 and begin == 0:
-            grid_copy(t).wait()
-        transform(t, begin, begin + half)
-        if unit == 0:
-            pl.semaphore_wait(barrier, nb - 1 + steps)
-            mom_send(0).start()
-        j = ends.get((t, begin + half))
-        if j is not None:
-            for peer in others:
-                piece_send(j, peer).start()
+        if unit == 2:
+            for j in range(2, grids):
+                grid_copy(j).wait()
+        for top in range(begin, begin + half, HEAD if unit == 0 else half):
+            stop = top + (HEAD if unit == 0 else half)
+            if unit == 0 and top == HEAD:
+                grid_copy(1).wait()
+            transform(t, top, stop)
+            if unit == 0 and top == 0:
+                pl.semaphore_wait(barrier, nb - 1 + steps)
+                mom_send(0).start()
+            j = ends.get((t, stop))
+            if j is not None:
+                for peer in others:
+                    piece_send(j, peer).start()
         if unit == 0:
             spread(goals[0])
             mom_add(0)
@@ -385,7 +394,9 @@
     for s in range(2, steps):
         jobs.append((z_due(0) + s, s, mom_add, (s,)))
         for c in range(chunks):
-            jobs.append((max(z_due(c + 2 * (s - 1)) + 2.4, 45.5 + (s - steps)), s, half_add, (c, s)))
+            due = z_due(chunks - 1) - 0.2 if s == steps - 1 else z_due(c)
+            due += 1.5 * (s - 1) + 2.5 * (c == chunks - 1)
+            jobs.append((due, s, half_add, (c, s)))
     jobs.append((28.0, 9, open_pieces, ()))
     for q in range(slices):
         jobs.append((32.0 + 22.5 * (q + 1) / slices, 10, flip_go, (q,)))
@@ -436,7 +447,17 @@
 def head_pieces(tiles):
     early = tiles // 2
     half = SUB // 2
-    return [(0, 0, half), (0, half, half)][: 2 * early] + [(t, 0, SUB) for t in range(1, early)]
+    first = [(0, top, HEAD) for top in range(0, half, HEAD)] + [(0, half, half)]
+    return (first if early else []) + [(t, 0, SUB) for t in range(1, early)]
+
+
+def grid_reads(tiles):
+    reads = [(0, 1, 0, HEAD), (0, 1, HEAD, SUB - HEAD)]
+    return reads + [(1, tiles - 1, 0, SUB)] * (tiles > 1)
+
+
+def res_reads(parts):
+    return [(0, 1)] + [(1, parts - 1)] * (parts > 1)
 
 
 def place_kernel(slices, spec_ref, comp_ref, recv_ref, spec_hbm, comp_hbm, spec_v, sem):
@@ -472,7 +493,7 @@
     slices = min(8, kept)
     steps = int(math.log2(nc))
     view = gridded.reshape(2, tiles, SUB, outer, LANES)
-    view = jnp.transpose(view, (0, 1, 3, 2, 4)).reshape(2, tiles, outer * SUB, LANES)
+    view = jnp.transpose(view, (0, 1, 3, 2, 4))
     vmem = pl.BlockSpec(memory_space=pltpu.VMEM)
     hbm = pl.BlockSpec(memory_space=pl.ANY)
     dma = pltpu.SemaphoreType.DMA
@@ -491,9 +512,9 @@
             *[pltpu.VMEM(c.shape, c.dtype) for c in consts],
             pltpu.SMEM(weight_index.shape, jnp.int32),
             pltpu.SMEM(weight_table.shape, jnp.float32),
-            pltpu.VMEM((2, tiles, outer * SUB, LANES), jnp.float32),
+            pltpu.VMEM((2, tiles, outer, SUB, LANES), jnp.float32),
             pltpu.VMEM((tiles, LANES * 2, SUB, outer), jnp.float32),
-            pltpu.VMEM((parts, count, SUB, columns), jnp.float32),
+            pltpu.VMEM((count, parts, SUB, columns), jnp.float32),
             pltpu.VMEM((parts * halves, nc, 3 * SUB, wide // halves), jnp.float32),
             pltpu.VMEM((steps, SUB, LANES), jnp.float32),
             pltpu.VMEM((steps, SUB, LANES), jnp.float32),
@@ -503,8 +524,8 @@
             ],
             dma((2,)),
             dma((bases + 1,)),
-            dma((tiles,)),
-            dma((parts,)),
+            dma((len(grid_reads(tiles)),)),
+            dma((len(res_reads(parts)),)),
             dma((1,)),
             dma((1,)),
             dma((slices,)),
@@ -517,7 +538,7 @@
             collective_id=0, has_side_effects=True, vmem_limit_bytes=58_000_000
         ),
         name="exchange",
-    )(weight_index, weight_table, *consts, residual, view)
+    )(weight_index, weight_table, *consts, residual.reshape(count, parts, SUB, columns), view)
     spectrum, components = pl.pallas_call(
         functools.partial(place_kernel, slices),
         out_shape=(

time: 55.4 us -> 54.7 us (0.987)
  Pallas kernels: 54.6 us -> 54 us
    pallas_call x1, Pallas kernels: 52.4 us -> 51.7 us  [local(): pl.pallas_call(functools.partial(exchange_kernel, nc, nb, bases), out_sha...]
where the time goes in v4:
time: 54.7 us; the launch traced here: 54.6 us
  Pallas kernels  54 us (99%)
  between operations  0.64 us (1%)
    pallas_call x1, Pallas kernels, local(): pl.pallas_call(functools.partial(exchange_kernel, nc, nb, bases), out_sha...  51.7 us
    pallas_call x1, Pallas kernels, local(): pl.pallas_call(functools.partial(place_kernel, slices), out_shape=(jax.Sh...  2.23 us

profile of v4, /device:TPU:0, one launch (start us, length us, event | category | flops | bytes accessed | tf_op | source)
XLA Modules:
  0.0 54.6 jit_solution(11155123947680452716)
XLA Ops:
  0.6 51.7 %exchange.1 = (f32[2,1,4096,128]{3,2,1,0:T(8,128)S(1)}, f32[3,24,2048]{2,1,0:T(8,128)S(1)}, f32[16,64,8,128]{3,2,1,0:T(8,128)S(1)}) custom-call(s32[8]{0:T(128)} %idx_hbm.1, f32[16]{0:T(128)} %tab_hbm.1, f32[2,128,128]{2,1,0:T(8,128)} %constant.4.clone.rest_0_, bf16[256,768]{1,0:T(8,128)(2,1)} %constant.5.clone.rest_1_, f32[8,3,8,16384]{3,2,1,0:T(8,128)} %bitcast.4, ...), custom_call_target="tpu_custom_call" | custom-call | tf_op jit(solution)/shard_map/exchange/pallas_call | solution.py:506
  52.4 2.2 %place.1 = (f32[2,1,4096,128]{3,2,1,0:T(8,128)}, f32[3,24,2048]{2,1,0:T(8,128)}) custom-call(f32[2,1,4096,128]{3,2,1,0:T(8,128)S(1)} %get-tuple-element.7.spec_ref, f32[3,24,2048]{2,1,0:T(8,128)S(1)} %get-tuple-element.8.comp_ref, f32[16,64,8,128]{3,2,1,0:T(8,128)S(1)} %get-tuple-element.9.recv_ref), custom_call_target="tpu_custom_call" | custom-call | tf_op jit(solution)/shard_map/place/pallas_call | solution.py:542

commit v5 on v4

--- a/solution.py
+++ b/solution.py
@@ -12,7 +12,6 @@
 MESH = pl.DeviceIdType.MESH
 LANES = 128
 SUB = 8
-AHEAD = 3
 HEAD = 2
 
 
@@ -51,14 +50,14 @@
 
 
 def exchange_kernel(nc, nb, bases, idx_hbm, tab_hbm, *rest):
-    steps = int(math.log2(nc))
+    line = nc // 2
     tables_hbm, (res_hbm, grid_hbm) = rest[: bases + 1], rest[bases + 1 : bases + 3]
     spec_ref, comp_ref, recv_v = rest[bases + 3 : bases + 6]
     rest = rest[bases + 6 :]
     tables_v, rest = rest[: bases + 1], rest[bases + 1 :]
-    (idx_ref, tab_ref, grid_v, out_v, res_v, part_v, mom_v, mom_land) = rest[:8]
-    lands = rest[8 : 8 + steps]
-    (idx_sem, tab_sem, grid_sem, res_sem, bs_sem, er_sem, lr_sem, rs_sem, rr_sem, ms_sem, mr_sem) = rest[8 + steps :]
+    (idx_ref, tab_ref, grid_v, out_v, res_v, part_v, pair_v, land_v, mom_v, mom_land) = rest[:10]
+    (idx_sem, tab_sem, grid_sem, res_sem, bs_sem, er_sem, lr_sem) = rest[10:17]
+    (zs_sem, pair_sem, fw_sem, fin_sem, ms_sem, mr_sem, ok_sem) = rest[17:]
     turn_v, first_v, second_v = tables_v[0], tables_v[1], tables_v[-1]
     chan = lax.axis_index("chan")
     band = lax.axis_index("band")
@@ -66,8 +65,8 @@
     kept = LANES // nb
     count, parts = res_v.shape[0], res_v.shape[1]
     wide = part_v.shape[3]
-    chunks = part_v.shape[0]
-    cuts = chunks // parts
+    cells = chunk_list(parts, wide)
+    chunks = len(cells)
     early = tiles // 2
     late = tiles - early
     pieces = head_pieces(tiles)
@@ -83,16 +82,13 @@
         return pltpu.make_async_copy(grid_hbm.at[at], grid_v.at[at], grid_sem.at[j])
 
     def res_copy(j):
-        first, count = res_reads(parts)[j]
-        at = pl.ds(first, count)
-        return pltpu.make_async_copy(res_hbm.at[:, at], res_v.at[:, at], res_sem.at[j])
-
-    bits = [(chan // (1 << s)) % 2 for s in range(steps)]
-    partners = [chan + (1 - 2 * bits[s]) * (1 << s) for s in range(steps)]
+        first, many, begin, size = res_reads(parts, wide)[j]
+        at = (slice(None), pl.ds(first, many), slice(None), pl.ds(begin // LANES, size // LANES))
+        return pltpu.make_async_copy(res_hbm.at[at], res_v.at[at], res_sem.at[j])
+
+    core, place = chan % 2, chan // 2
+    mate = chan + 1 - 2 * core
     others = [crossed(band, nb, mask) for mask in range(nb - 1, 0, -1)]
-    starts = [0]
-    for s in range(steps):
-        starts.append(starts[s] + bits[s] * (nc >> (s + 1)))
 
     small = [
         pltpu.make_async_copy(idx_hbm, idx_ref, idx_sem.at[0]),
@@ -107,8 +103,11 @@
     barrier = pltpu.get_barrier_semaphore()
     for peer in others:
         pl.semaphore_signal(barrier, inc=1, device_id=(chan, peer), device_id_type=MESH)
-    for s in range(steps):
-        pl.semaphore_signal(barrier, inc=1, device_id=(partners[s], band), device_id_type=MESH)
+    pl.semaphore_signal(barrier, inc=1, device_id=(mate, band), device_id_type=MESH)
+
+    @pl.when(place < line - 1)
+    def _():
+        pl.semaphore_signal(barrier, inc=1, device_id=(chan + 2, band), device_id_type=MESH)
 
     def transform(t, begin, stop):
         def pair(i, carry):
@@ -188,135 +187,187 @@
     coeffs = []
 
     def weigh(c):
-        step = 512 if wide % 512 == 0 else LANES
+        part, begin, size = cells[c]
 
         def one(j, carry):
-            spot = 0
-            for s in range(steps):
-                spot = spot + ((j // (1 << s)) % 2) * (1 << (steps - 1 - s))
-            for q in range(wide // step):
-                col = pl.multiple_of((j * cuts + c % cuts) * wide + q * step, LANES)
+            spot = (j % 2) * line + j // 2
+            for q in range(begin // LANES, (begin + size) // LANES):
                 sums = [None] * 3
                 for ch in range(count):
-                    x = res_v[ch, c // cuts, :, pl.ds(col, step)]
+                    x = res_v[ch, part, j, q]
                     for t in range(3):
                         term = coeffs[ch][t] * x
                         sums[t] = term if ch == 0 else sums[t] + term
                 for t in range(3):
-                    part_v[c, spot, pl.ds(t * SUB, SUB), pl.ds(q * step, step)] = sums[t]
+                    part_v[part, spot, pl.ds(t * SUB, SUB), pl.ds(q * LANES, LANES)] = sums[t]
             return carry
 
         lax.fori_loop(0, nc, one, 0)
-
-    batches = batch_list(chunks, steps)
-
-    def batch_of(c, s):
-        for spot, (step, first, last) in enumerate(batches):
-            if step == s and first <= c < last:
-                return spot, first, last
 
     def landed(ref, sem):
         pltpu.make_async_copy(ref, ref, sem).wait()
 
-    def half_send(c, s):
-        size = nc >> (s + 1)
-        begin = starts[s] + (1 - bits[s]) * size
+    def pair_send(c):
+        part, left, width = cells[c]
+        at = pl.ds(left, width)
         return pltpu.make_async_remote_copy(
-            src_ref=part_v.at[c, pl.ds(begin, size)],
-            dst_ref=lands[s].at[c],
-            send_sem=rs_sem.at[0],
-            recv_sem=rr_sem.at[batch_of(c, s)[0]],
-            device_id=(partners[s], band),
+            src_ref=part_v.at[part, pl.ds((1 - core) * line, line), :, at],
+            dst_ref=pair_v.at[part, :, :, at],
+            send_sem=zs_sem.at[0],
+            recv_sem=pair_sem.at[c],
+            device_id=(mate, band),
             device_id_type=MESH,
         )
 
-    def mom_send(s):
+    def pair_add(c):
+        part, left, width = cells[c]
+        at = pl.ds(left, width)
+        landed(pair_v.at[part, :, :, at], pair_sem.at[c])
+
+        def one(k, carry):
+            part_v[part, core * line + k, :, at] = part_v[part, core * line + k, :, at] + pair_v[part, k, :, at]
+            return carry
+
+        lax.fori_loop(0, line, one, 0)
+
+    def facing(hop):
+        return (place == line - 1 - hop).astype(jnp.int32)
+
+    def line_send(p, hop, c):
+        part, left, width = cells[c]
+        at = pl.ds(left, width)
+        down = facing(hop)
+        spot = core * line + line - 1 - p + down * (2 * p - line + 1)
+        last = hop + 1 == line - 1 - p
+        sem = fin_sem.at[down * parts + part] if last else fw_sem.at[(down * (line - 2) + p) * chunks + c]
         return pltpu.make_async_remote_copy(
-            src_ref=mom_v.at[s],
-            dst_ref=mom_land.at[s],
-            send_sem=ms_sem.at[0],
-            recv_sem=mr_sem.at[s],
-            device_id=(partners[s], band),
+            src_ref=part_v.at[part, spot, :, at],
+            dst_ref=land_v.at[down * (line - 1) + p, part, :, at],
+            send_sem=zs_sem.at[0],
+            recv_sem=sem,
+            device_id=(chan + 2 - 4 * down, band),
             device_id_type=MESH,
         )
 
+    def set_out(p, c):
+        @pl.when((place == 0) | (place == line - 1))
+        def _():
+            line_send(p, 0, c).start()
+
+    def forward(p, hop, c):
+        @pl.when((place == hop) | (place == line - 1 - hop))
+        def _():
+            part, left, width = cells[c]
+            at = pl.ds(left, width)
+            down = facing(hop)
+            spot = core * line + line - 1 - p + down * (2 * p - line + 1)
+            row = down * (line - 1) + p
+            landed(land_v.at[row, part, :, at], fw_sem.at[(down * (line - 2) + p) * chunks + c])
+            part_v[part, spot, :, at] = part_v[part, spot, :, at] + land_v[row, part, :, at]
+            line_send(p, hop, c).start()
+
+    def finish(part):
+        own = core * line + place
+
+        @pl.when(place > 0)
+        def _():
+            row = line - 1 - place
+            landed(land_v.at[row, part], fin_sem.at[part])
+            part_v[part, own] = part_v[part, own] + land_v[row, part]
+
+        @pl.when(place < line - 1)
+        def _():
+            row = line - 1 + place
+            landed(land_v.at[row, part], fin_sem.at[parts + part])
+            part_v[part, own] = part_v[part, own] + land_v[row, part]
+
+        aa, ab, ac, bb, bc, cc = solved
+        table = ((aa, ab, ac), (ab, bb, bc), (ac, bc, cc))
+        for q in range(wide // LANES):
+            at = pl.ds(q * LANES, LANES)
+            tay = [part_v[part, own, pl.ds(t * SUB, SUB), at] for t in range(3)]
+            for t, row in enumerate(table):
+                comp_ref[t, pl.ds(part * SUB, SUB), at] = row[0] * tay[0] + row[1] * tay[1] + row[2] * tay[2]
+
+    def mom_send(way):
+        return pltpu.make_async_remote_copy(
+            src_ref=mom_v.at[(0, 2, 3)[way]],
+            dst_ref=mom_land.at[way],
+            send_sem=ms_sem.at[way],
+            recv_sem=mr_sem.at[way],
+            device_id=((mate, chan + 2, chan - 2)[way], band),
+            device_id_type=MESH,
+        )
+
+    def mom_pair():
+        mom_send(0).wait_recv()
+        mom_v[1] = mom_v[0] + mom_land[0]
+
+        @pl.when(place < line - 1)
+        def _():
+            pl.semaphore_wait(ok_sem, 1)
+
+        mom_hop(0)
+
+    def mom_hop(hop):
+        for way, from_end in ((1, place), (2, line - 1 - place)):
+
+            @pl.when(from_end == hop)
+            def _(way=way):
+                if hop:
+                    mom_send(way).wait_recv()
+                    mom_v[way + 1] = mom_v[1] + mom_land[way]
+                else:
+                    mom_v[way + 1] = mom_v[1]
+                if hop < line - 1:
+                    mom_send(way).start()
+
     solved = []
 
-    def mom_add(s):
-        mom_send(s).wait_recv()
-        moment = mom_v[s] + mom_land[s]
-        if s < steps - 1:
-            mom_v[s + 1] = moment
-            mom_send(s + 1).start()
-            return
-        for entry in inverse_rows(moment):
+    def mom_close():
+        mom_hop(line - 1)
+        mom_v[4] = mom_v[2]
+
+        @pl.when(place < line - 1)
+        def _():
+            mom_v[4] = mom_v[2] + mom_land[2]
+
+        for entry in inverse_rows(mom_v[4]):
             solved.append(jnp.broadcast_to(entry, (SUB, LANES)))
 
-    def half_add(c, s, send=True):
-        spot, first, last = batch_of(c, s)
-        if c == first:
-            landed(lands[s].at[pl.ds(first, last - first)], rr_sem.at[spot])
-        size = nc >> (s + 1)
-        if s == steps - 1:
-            aa, ab, ac, bb, bc, cc = solved
-            table = ((aa, ab, ac), (ab, bb, bc), (ac, bc, cc))
-            for q in range(wide // LANES):
-                at = pl.ds(q * LANES, LANES)
-                tay = [
-                    part_v[c, starts[s + 1], pl.ds(t * SUB, SUB), at] + lands[s][c, 0, pl.ds(t * SUB, SUB), at]
-                    for t in range(3)
-                ]
-                for t, row in enumerate(table):
-                    comp_ref[t, pl.ds(c // cuts * SUB, SUB), pl.ds(c % cuts * wide + q * LANES, LANES)] = (
-                        row[0] * tay[0] + row[1] * tay[1] + row[2] * tay[2]
-                    )
-            return
-        half = size // 2
-        for mine in (1 - bits[s + 1], bits[s + 1]):
-            for q in range(half):
-                at = mine * half + q
-                part_v[c, starts[s + 1] + at] = part_v[c, starts[s + 1] + at] + lands[s][c, at]
-            if send and mine is not bits[s + 1]:
-                half_send(c, s + 1).start()
-
-    ahead = min(AHEAD, chunks)
-    moved = weighed = added = 0
-    issued = ahead
-
-    def advance(target, ahead=AHEAD):
-        nonlocal moved, issued
-        while moved < min(target, chunks):
-            half_add(moved, 1)
-            moved += 1
-            while issued < min(moved + ahead, chunks):
-                half_send(issued, 1).start()
-                issued += 1
+    weighed = added = 0
+
+    def ready(c):
+        for j, (first, _, begin, _) in enumerate(res_reads(parts, wide)):
+            if cells[c][:2] == (first, begin):
+                res_copy(j).wait()
+        weigh(c)
 
     def spread(target):
         nonlocal weighed
         while weighed < min(target, chunks):
-            for j, (first, _) in enumerate(res_reads(parts)):
-                if weighed == first * cuts:
-                    res_copy(j).wait()
-            weigh(weighed)
-            half_send(weighed, 0).start()
+            ready(weighed)
+            pair_send(weighed).start()
             weighed += 1
 
     def gather(target):
         nonlocal added
         while added < min(target, chunks):
-            half_add(added, 0, send=added < ahead)
+            pair_add(added)
+            for p, c in leaving:
+                if added == c and (p == 0 or c < 2) or added == chunks - 1 > 1 and p > 0 and c >= 2:
+                    set_out(p, c)
             added += 1
 
     for j in range(bases, -1, -1):
         table_copy(j).wait()
     grid_copy(0).wait()
-    grids, reads = len(grid_reads(tiles)), len(res_reads(parts))
+    grids, reads = len(grid_reads(tiles)), len(res_reads(parts, wide))
     for j in range(max(grids - 1, reads)):
+        if j < reads:
+            res_copy(j).start()
         if j + 1 < grids:
             grid_copy(j + 1).start()
-        if j < reads:
-            res_copy(j).start()
 
     for copy in small:
         copy.wait()
@@ -334,14 +385,39 @@
             moments[j] = moments[j] + power
             power = power * offset
         coeffs.append(trio)
-    line = lax.broadcasted_iota(jnp.int32, (SUB, LANES), 0)
+    level = lax.broadcasted_iota(jnp.int32, (SUB, LANES), 0)
     tile = jnp.zeros((SUB, LANES), jnp.float32)
     for j in range(5):
-        tile = jnp.where(line == j, moments[j], tile)
+        tile = jnp.where(level == j, moments[j], tile)
     mom_v[0] = tile
 
+    def open_pieces():
+        landed(recv_v.at[pl.ds(0, (nb - 1) * early)], er_sem.at[0])
+
+    def flip_go(q):
+        landed(recv_v.at[pl.ds(0, (nb - 1) * late), pl.ds(0, span * 2)], lr_sem.at[q])
+        if q < slices - 1:
+            flip(q)
+
+    leaving = [(p, c) for c in range(min(2, chunks)) for p in range(line - 1)]
+    leaving += [(p, c) for p in range(line - 1) for c in range(2, chunks)]
+    jobs, clock = [], 9.0
+    for p, c in leaving:
+        takes = 12.6 * cells[c][2] / (parts * wide)
+        clock += takes
+        for hop in range(1, line - 1 - p):
+            jobs.append((clock + (hop - 1) * (2.5 + takes), hop, forward, (p, hop, c)))
+    for hop in range(1, line - 1):
+        jobs.append((9.0 + 5.0 * hop, 0, mom_hop, (hop,)))
+    jobs.append((30.0, 0, mom_close, ()))
+    for part in range(parts):
+        jobs.append((48.0 - 4.2 * (parts - 1 - part), 20, finish, (part,)))
+    jobs.append((31.5, 9, open_pieces, ()))
+    for q in range(slices):
+        jobs.append((33.0 + 22.5 * (q + 1) / slices, 10, flip_go, (q,)))
+    jobs.sort(key=lambda job: job[:2])
+
     half = SUB // 2
-    goals = [last for step, _, last in batches if step == 0]
     ends = {(t, begin + size): j for j, (t, begin, size) in enumerate(pieces)}
     for unit in range(2 * tiles):
         t, begin = unit // 2, unit % 2 * half
@@ -354,23 +430,28 @@
                 grid_copy(1).wait()
             transform(t, top, stop)
             if unit == 0 and top == 0:
-                pl.semaphore_wait(barrier, nb - 1 + steps)
-                mom_send(0).start()
+                pl.semaphore_wait(barrier, nb + (place > 0).astype(jnp.int32))
+
+                @pl.when(place > 0)
+                def _():
+                    pl.semaphore_signal(ok_sem, inc=1, device_id=(chan - 2, band), device_id_type=MESH)
+
             j = ends.get((t, stop))
             if j is not None:
                 for peer in others:
                     piece_send(j, peer).start()
+            if unit == 0 and top == 0:
+                mom_send(0).start()
         if unit == 0:
-            spread(goals[0])
-            mom_add(0)
-            spread(goals[1])
-            gather(goals[1])
+            spread(2)
+            mom_pair()
+            gather(1)
         else:
-            gather(goals[min(unit, len(goals) - 1)])
-            spread(goals[min(unit + 1, len(goals) - 1)])
-            if unit == 2:
-                mom_add(1)
-            advance((0, 0, 1, 2, 3, 3, 4, 5)[min(unit, 7)])
+            gather(unit + 1)
+            spread(unit + 2)
+        while jobs and jobs[0][0] < 7.5 + 2.05 * unit:
+            _, _, work, args = jobs.pop(0)
+            work(*args)
         if begin:
             keep(t)
     for q in range(slices):
@@ -379,34 +460,18 @@
     spread(chunks)
     gather(chunks)
 
-    def open_pieces():
-        landed(recv_v.at[pl.ds(0, (nb - 1) * early)], er_sem.at[0])
-
-    def flip_go(q):
-        landed(recv_v.at[pl.ds(0, (nb - 1) * late), pl.ds(0, span * 2)], lr_sem.at[q])
-        if q < slices - 1:
-            flip(q)
-
-    def z_due(c):
-        return 7.2 + 38.0 * (c + 1) / chunks
-
-    jobs = [(z_due(c), 1, advance, (c + 1, 2)) for c in range(moved, chunks)]
-    for s in range(2, steps):
-        jobs.append((z_due(0) + s, s, mom_add, (s,)))
-        for c in range(chunks):
-            due = z_due(chunks - 1) - 0.2 if s == steps - 1 else z_due(c)
-            due += 1.5 * (s - 1) + 2.5 * (c == chunks - 1)
-            jobs.append((due, s, half_add, (c, s)))
-    jobs.append((28.0, 9, open_pieces, ()))
-    for q in range(slices):
-        jobs.append((32.0 + 22.5 * (q + 1) / slices, 10, flip_go, (q,)))
-    jobs.sort(key=lambda job: job[:2])
     for _, _, work, args in jobs:
         work(*args)
 
     def drain_z():
-        landed(mom_v, ms_sem.at[0])
-        landed(part_v.at[:, pl.ds(0, nc - 1)], rs_sem.at[0])
+        mom_send(0).wait_send()
+        for way, sends in ((1, place < line - 1), (2, place > 0)):
+
+            @pl.when(sends)
+            def _(way=way):
+                mom_send(way).wait_send()
+
+        landed(part_v.at[:, pl.ds(0, nc - 1)], zs_sem.at[0])
 
     def drain_band():
         landed(recv_v.at[pl.ds(0, (nb - 1) * tiles)], bs_sem.at[0])
@@ -435,13 +500,9 @@
     lax.fori_loop(0, span, one, 0, unroll=2 if span % 2 == 0 else 1)
 
 
-def batch_list(chunks, steps):
-    batches = [(0, 0, 1), (0, 1, min(3, chunks))]
-    batches += [(0, c, min(c + 3, chunks)) for c in range(3, chunks, 3)]
-    for s in range(1, steps - 1):
-        batches += [(s, c, c + 1) for c in range(chunks)]
-    cuts = sorted({0, max(chunks - 4, 0), chunks - 1, chunks})
-    return batches + [(steps - 1, a, b) for a, b in zip(cuts, cuts[1:])]
+def chunk_list(parts, wide):
+    first = wide // 4
+    return [(0, 0, first), (0, first, wide - first)] + [(part, 0, wide) for part in range(1, parts)]
 
 
 def head_pieces(tiles):
@@ -456,8 +517,9 @@
     return reads + [(1, tiles - 1, 0, SUB)] * (tiles > 1)
 
 
-def res_reads(parts):
-    return [(0, 1)] + [(1, parts - 1)] * (parts > 1)
+def res_reads(parts, wide):
+    first = wide // 4
+    return [(0, 1, 0, first), (0, 1, first, wide - first), (1, parts - 1, 0, wide)]
 
 
 def place_kernel(slices, spec_ref, comp_ref, recv_ref, spec_hbm, comp_hbm, spec_v, sem):
@@ -488,12 +550,13 @@
     outer = length // LANES
     tiles, parts = rows // SUB, row_count // SUB
     wide = columns // nc
-    halves = 4
     kept = LANES // nb
     slices = min(8, kept)
-    steps = int(math.log2(nc))
+    line = nc // 2
     view = gridded.reshape(2, tiles, SUB, outer, LANES)
     view = jnp.transpose(view, (0, 1, 3, 2, 4))
+    pixels = residual.reshape(count, parts, SUB, nc, wide // LANES, LANES)
+    pixels = jnp.transpose(pixels, (0, 1, 3, 4, 2, 5))
     vmem = pl.BlockSpec(memory_space=pltpu.VMEM)
     hbm = pl.BlockSpec(memory_space=pl.ANY)
     dma = pltpu.SemaphoreType.DMA
@@ -502,7 +565,7 @@
     shape_spec = (2, 1, kept * outer, nb * rows)
     shape_comp = (3, row_count, wide)
     shape_recv = (nb * tiles, kept * 2, SUB, outer)
-    batches = len(batch_list(parts * halves, steps))
+    chunks = len(chunk_list(parts, wide))
     held = pl.pallas_call(
         functools.partial(exchange_kernel, nc, nb, bases),
         out_shape=tuple(pltpu.VMEM(shape, jnp.float32) for shape in (shape_spec, shape_comp, shape_recv)),
@@ -514,31 +577,32 @@
             pltpu.SMEM(weight_table.shape, jnp.float32),
             pltpu.VMEM((2, tiles, outer, SUB, LANES), jnp.float32),
             pltpu.VMEM((tiles, LANES * 2, SUB, outer), jnp.float32),
-            pltpu.VMEM((count, parts, SUB, columns), jnp.float32),
-            pltpu.VMEM((parts * halves, nc, 3 * SUB, wide // halves), jnp.float32),
-            pltpu.VMEM((steps, SUB, LANES), jnp.float32),
-            pltpu.VMEM((steps, SUB, LANES), jnp.float32),
-            *[
-                pltpu.VMEM((parts * halves, nc >> (s + 1), 3 * SUB, wide // halves), jnp.float32)
-                for s in range(steps)
-            ],
+            pltpu.VMEM(pixels.shape, jnp.float32),
+            pltpu.VMEM((parts, nc, 3 * SUB, wide), jnp.float32),
+            pltpu.VMEM((parts, line, 3 * SUB, wide), jnp.float32),
+            pltpu.VMEM((2 * (line - 1), parts, 3 * SUB, wide), jnp.float32),
+            pltpu.VMEM((5, SUB, LANES), jnp.float32),
+            pltpu.VMEM((3, SUB, LANES), jnp.float32),
             dma((2,)),
             dma((bases + 1,)),
             dma((len(grid_reads(tiles)),)),
-            dma((len(res_reads(parts)),)),
+            dma((len(res_reads(parts, wide)),)),
             dma((1,)),
             dma((1,)),
             dma((slices,)),
             dma((1,)),
-            dma((batches,)),
-            dma((1,)),
-            dma((steps,)),
+            dma((chunks,)),
+            dma((2 * (line - 2) * chunks,)),
+            dma((2 * parts,)),
+            dma((3,)),
+            dma((3,)),
+            pltpu.SemaphoreType.REGULAR,
         ],
         compiler_params=pltpu.CompilerParams(
             collective_id=0, has_side_effects=True, vmem_limit_bytes=58_000_000
         ),
         name="exchange",
-    )(weight_index, weight_table, *consts, residual.reshape(count, parts, SUB, columns), view)
+    )(weight_index, weight_table, *consts, pixels, view)
     spectrum, components = pl.pallas_call(
         functools.partial(place_kernel, slices),
         out_shape=(

time: 54.7 us -> 54.2 us (level)
  no operation moved by 1% of the time
where the time goes in v5:
time: 54.2 us; the launch traced here: 54.1 us
  Pallas kernels  53.5 us (99%)
  between operations  0.64 us (1%)
    pallas_call x1, Pallas kernels, local(): pl.pallas_call(functools.partial(exchange_kernel, nc, nb, bases), out_sha...  51.2 us
    pallas_call x1, Pallas kernels, local(): pl.pallas_call(functools.partial(place_kernel, slices), out_shape=(jax.Sh...  2.23 us

profile of v5, /device:TPU:0, one launch (start us, length us, event | category | flops | bytes accessed | tf_op | source)
XLA Modules:
  0.0 54.1 jit_solution(6510641785726772070)
XLA Ops:
  0.6 51.2 %exchange.1 = (f32[2,1,4096,128]{3,2,1,0:T(8,128)S(1)}, f32[3,24,2048]{2,1,0:T(8,128)S(1)}, f32[16,64,8,128]{3,2,1,0:T(8,128)S(1)}) custom-call(s32[8]{0:T(128)} %idx_hbm.1, f32[16]{0:T(128)} %tab_hbm.1, f32[2,128,128]{2,1,0:T(8,128)} %constant.4.clone.rest_0_, bf16[256,768]{1,0:T(8,128)(2,1)} %constant.5.clone.rest_1_, f32[8,3,8,16,8,128]{5,4,3,2,1,0:T(8,128)} %bitcast.6, ...), custom_call_target="tpu_custom_call" | custom-call | tf_op jit(solution)/shard_map/exchange/pallas_call | solution.py:569
  51.9 2.2 %place.1 = (f32[2,1,4096,128]{3,2,1,0:T(8,128)}, f32[3,24,2048]{2,1,0:T(8,128)}) custom-call(f32[2,1,4096,128]{3,2,1,0:T(8,128)S(1)} %get-tuple-element.7.spec_ref, f32[3,24,2048]{2,1,0:T(8,128)S(1)} %get-tuple-element.8.comp_ref, f32[16,64,8,128]{3,2,1,0:T(8,128)S(1)} %get-tuple-element.9.recv_ref), custom_call_target="tpu_custom_call" | custom-call | tf_op jit(solution)/shard_map/place/pallas_call | solution.py:606

commit v6 on v5

--- a/solution.py
+++ b/solution.py
@@ -70,8 +70,9 @@
     early = tiles // 2
     late = tiles - early
     pieces = head_pieces(tiles)
-    slices = lr_sem.shape[0]
+    slices = min(8, kept)
     span = kept // slices
+    joined = slices - lr_sem.shape[0] + 1
 
     def table_copy(j):
         return pltpu.make_async_copy(tables_hbm[j], tables_v[j], tab_sem.at[j])
@@ -173,7 +174,7 @@
             src_ref=out_v.at[pl.ds(early, late), pl.ds((peer * kept + q * span) * 2, span * 2)],
             dst_ref=recv_v.at[pl.ds(band * tiles + early, late), pl.ds(q * span * 2, span * 2)],
             send_sem=bs_sem.at[0],
-            recv_sem=lr_sem.at[q],
+            recv_sem=lr_sem.at[max(q - joined + 1, 0)],
             device_id=(chan, peer),
             device_id_type=MESH,
         )
@@ -239,7 +240,7 @@
         down = facing(hop)
         spot = core * line + line - 1 - p + down * (2 * p - line + 1)
         last = hop + 1 == line - 1 - p
-        sem = fin_sem.at[down * parts + part] if last else fw_sem.at[(down * (line - 2) + p) * chunks + c]
+        sem = fin_sem.at[down * parts + part] if last else fw_sem.at[(down * (line - 2) + p) * parts + part]
         return pltpu.make_async_remote_copy(
             src_ref=part_v.at[part, spot, :, at],
             dst_ref=land_v.at[down * (line - 1) + p, part, :, at],
@@ -257,14 +258,15 @@
     def forward(p, hop, c):
         @pl.when((place == hop) | (place == line - 1 - hop))
         def _():
-            part, left, width = cells[c]
-            at = pl.ds(left, width)
+            part = cells[c][0]
             down = facing(hop)
             spot = core * line + line - 1 - p + down * (2 * p - line + 1)
             row = down * (line - 1) + p
-            landed(land_v.at[row, part, :, at], fw_sem.at[(down * (line - 2) + p) * chunks + c])
-            part_v[part, spot, :, at] = part_v[part, spot, :, at] + land_v[row, part, :, at]
-            line_send(p, hop, c).start()
+            landed(land_v.at[row, part], fw_sem.at[(down * (line - 2) + p) * parts + part])
+            part_v[part, spot] = part_v[part, spot] + land_v[row, part]
+            for k, cell in enumerate(cells):
+                if cell[0] == part:
+                    line_send(p, hop, k).start()
 
     def finish(part):
         own = core * line + place
@@ -395,9 +397,13 @@
         landed(recv_v.at[pl.ds(0, (nb - 1) * early)], er_sem.at[0])
 
     def flip_go(q):
-        landed(recv_v.at[pl.ds(0, (nb - 1) * late), pl.ds(0, span * 2)], lr_sem.at[q])
-        if q < slices - 1:
-            flip(q)
+        if q < joined - 1:
+            return
+        first = 0 if q == joined - 1 else q
+        many = q + 1 - first
+        landed(recv_v.at[pl.ds(0, (nb - 1) * late), pl.ds(0, many * span * 2)], lr_sem.at[max(q - joined + 1, 0)])
+        for k in range(first, min(q + 1, slices - 1)):
+            flip(k)
 
     leaving = [(p, c) for c in range(min(2, chunks)) for p in range(line - 1)]
     leaving += [(p, c) for p in range(line - 1) for c in range(2, chunks)]
@@ -405,7 +411,7 @@
     for p, c in leaving:
         takes = 12.6 * cells[c][2] / (parts * wide)
         clock += takes
-        for hop in range(1, line - 1 - p):
+        for hop in range(1, line - 1 - p if c else 1):
             jobs.append((clock + (hop - 1) * (2.5 + takes), hop, forward, (p, hop, c)))
     for hop in range(1, line - 1):
         jobs.append((9.0 + 5.0 * hop, 0, mom_hop, (hop,)))
@@ -589,10 +595,10 @@
             dma((len(res_reads(parts, wide)),)),
             dma((1,)),
             dma((1,)),
-            dma((slices,)),
+            dma((slices - slices // 2 + 1,)),
             dma((1,)),
             dma((chunks,)),
-            dma((2 * (line - 2) * chunks,)),
+            dma((2 * (line - 2) * parts,)),
             dma((2 * parts,)),
             dma((3,)),
             dma((3,)),

time: 54.2 us -> 54.2 us (level)
  no operation moved by 1% of the time
where the time goes in v6:
time: 54.2 us; the launch traced here: 54 us
  Pallas kernels  53.4 us (99%)
  between operations  0.64 us (1%)
    pallas_call x1, Pallas kernels, local(): pl.pallas_call(functools.partial(exchange_kernel, nc, nb, bases), out_sha...  51.2 us
    pallas_call x1, Pallas kernels, local(): pl.pallas_call(functools.partial(place_kernel, slices), out_shape=(jax.Sh...  2.23 us

profile of v6, /device:TPU:0, one launch (start us, length us, event | category | flops | bytes accessed | tf_op | source)
XLA Modules:
  0.0 54.0 jit_solution(7055135303571230688)
XLA Ops:
  0.6 51.2 %exchange.1 = (f32[2,1,4096,128]{3,2,1,0:T(8,128)S(1)}, f32[3,24,2048]{2,1,0:T(8,128)S(1)}, f32[16,64,8,128]{3,2,1,0:T(8,128)S(1)}) custom-call(s32[8]{0:T(128)} %idx_hbm.1, f32[16]{0:T(128)} %tab_hbm.1, f32[2,128,128]{2,1,0:T(8,128)} %constant.4.clone.rest_0_, bf16[256,768]{1,0:T(8,128)(2,1)} %constant.5.clone.rest_1_, f32[8,3,8,16,8,128]{5,4,3,2,1,0:T(8,128)} %bitcast.6, ...), custom_call_target="tpu_custom_call" | custom-call | tf_op jit(solution)/shard_map/exchange/pallas_call | solution.py:575
  51.8 2.2 %place.1 = (f32[2,1,4096,128]{3,2,1,0:T(8,128)}, f32[3,24,2048]{2,1,0:T(8,128)}) custom-call(f32[2,1,4096,128]{3,2,1,0:T(8,128)S(1)} %get-tuple-element.7.spec_ref, f32[3,24,2048]{2,1,0:T(8,128)S(1)} %get-tuple-element.8.comp_ref, f32[16,64,8,128]{3,2,1,0:T(8,128)S(1)} %get-tuple-element.9.recv_ref), custom_call_target="tpu_custom_call" | custom-call | tf_op jit(solution)/shard_map/place/pallas_call | solution.py:612
